TPU v7x, 32 devices: a whole 2x2x4 slice. The times are simulated.
32 devices in a mesh: pool: 4 (over y, core), ga: 8 (over z, x).
Axes of the slice: x: 2, y: 2, z: 4, core: 2. Of those that a mesh axis runs over, the one named last changes fastest.
Arguments:
- coefficients: bfloat16 [4, 256, 2, 256, 128], P('pool', 'ga'), may hold values from -6 to 6
- stick_count: int32 [4, 8], P('pool', 'ga'), may hold values from 28 to 32, as said below
- dest_device: int32 [4, 256], P('pool', 'ga'), may hold values from -1 to 7, as said below
- dest_slot: int32 [4, 256], P('pool', 'ga'), may hold values from -1 to 31, as said below
- source_stick: int32 [4, 256], P('pool', 'ga'), may hold values from -1 to 255, as said below
Outputs:
- margins: float32 [4, 2, 256, 256], P('pool', None, 'ga')
Inputs may be any that keep to these rules, and one draw needn't show every extreme that they name: Every k-point has a device whose 32 slots are all live; a device's live sticks are its first stick_count slots. `dest_device`: -1 exactly for sticks that land nowhere (among them all sticks that are not live); no device sends more than 8 of its sticks to one device, and some pair of devices reaches 8 for every k-point. `dest_slot`: -1 where dest_device is -1; the slots named are live slots of the layout of k-point q-1, no slot named twice. `source_stick`: the exact inverse of dest_device and dest_slot: a slot names a stick exactly when that stick names the slot, else -1.
All inputs are finite; a program needn't handle non-finite values.
Results may differ from a plain program's by a relative error of at most 0.0003.
Values may be sent and summed in bfloat16 or wider, within the bound.
No kernel may reach another device: no remote copies, remote signals or barrier semaphores. Data moves between devices by JAX's collectives and lax.ppermute only.
A program may use at most 64 MiB of HBM per device.

v0:
```python
import jax
import jax.numpy as jnp
from jax import lax
from jax.experimental import pallas as pl
from jax.experimental.pallas import tpu as pltpu
from jax.sharding import PartitionSpec as P


def swapped_with(value, distance):
    count = lax.axis_size("ga")
    return lax.ppermute(value, "ga", [(i, i ^ distance) for i in range(count)])


def to_previous_pool(value):
    count = lax.axis_size("pool")
    return lax.ppermute(value, "pool", [(i, (i - 1) % count) for i in range(count)])


def pack(x, groups, me):
    slots, _, bands, waves = x.shape
    part = waves // groups
    if part % 16:
        cut = x.reshape(slots, 2, bands, groups, part).transpose(3, 1, 0, 4, 2)
        return [lax.dynamic_index_in_dim(cut, me ^ d, 0, False) for d in range(groups)]
    step = 4 if slots % 4 == 0 else 1

    def body(select_ref, x_ref, *refs):
        outs, held, sem = refs[:groups], refs[groups], refs[groups + 1]
        copies = [
            pltpu.make_async_copy(
                x_ref.at[pl.ds(i * step, step)], held.at[pl.ds(i * step, step)], sem.at[i]
            )
            for i in range(slots // step)
        ]
        for copy in copies:
            copy.start()
        for i, copy in enumerate(copies):
            copy.wait()
            for s in range(i * step, (i + 1) * step):
                for c in range(2):
                    turned = lax.dot_general(
                        select_ref[...],
                        held[s, c],
                        (((1,), (1,)), ((), ())),
                        preferred_element_type=jnp.float32,
                    ).astype(jnp.bfloat16)
                    for d in range(groups):
                        outs[d][c, s] = turned[d * part : (d + 1) * part]

    row = jnp.arange(waves, dtype=jnp.int32)
    source = ((row // part) ^ me) * part + row % part
    select = (source[:, None] == row[None, :]).astype(jnp.bfloat16)
    near = pl.BlockSpec(memory_space=pltpu.VMEM)
    return pl.pallas_call(
        body,
        in_specs=[near, pl.BlockSpec(memory_space=pl.ANY)],
        out_specs=[near] * groups,
        out_shape=[jax.ShapeDtypeStruct((2, slots, part, bands), jnp.bfloat16)] * groups,
        scratch_shapes=[
            pltpu.VMEM((slots, 2, bands, waves), jnp.bfloat16),
            pltpu.SemaphoreType.DMA((slots // step,)),
        ],
        compiler_params=pltpu.CompilerParams(vmem_limit_bytes=24 << 20),
        cost_estimate=pl.CostEstimate(
            flops=4 * slots * waves * waves * bands, bytes_accessed=x.size * 4, transcendentals=0
        ),
    )(select, x)


def gathered(mine, groups):
    rows = mine[None]
    levels = []
    distance = groups // 2
    while distance:
        other = swapped_with(rows, distance)
        rows = jnp.stack([rows, other], axis=len(levels))
        levels.append(2)
        rows = rows.reshape(*levels, 1, mine.shape[0])
        distance //= 2
    return rows.reshape(groups, mine.shape[0])


def pair_lists(bra_info, ket_info, groups, slots, me):
    counts = bra_info[:, 0]
    maps = ket_info[:, 1:].reshape(groups, 3, slots)
    device, slot, anchor = (maps[:, i].reshape(groups * slots) for i in range(3))
    number = jnp.arange(groups * slots, dtype=jnp.int32)
    here = ((number // slots) ^ me) * slots + number % slots
    lands = jnp.where(device >= 0, device * slots + slot, -1)
    live = (number % slots).reshape(groups, slots) < counts[:, None]
    agreeing = (anchor[:, None] == here[None, :]) & (lands[None, :] == here[:, None])
    agreeing &= live.reshape(-1)[:, None]
    ket_of = jnp.max(jnp.where(agreeing, number[None, :], -1), axis=1)
    bra_of = jnp.max(jnp.where(agreeing, number[:, None], -1), axis=0)
    return ket_of, bra_of


def multiply_plainly(bras, kets, ket_of, me, groups, scale):
    _, _, _, bands = bras[0].shape
    bra = jnp.concatenate(bras, axis=1)
    ket = jnp.concatenate(kets, axis=1)[:, jnp.maximum(ket_of, 0)]
    ket = jnp.where((ket_of >= 0)[None, :, None, None], ket, jnp.zeros_like(ket))

    def dot(a, b):
        return jnp.einsum("trm,trn->mn", bra[a], ket[b], preferred_element_type=jnp.float32)

    total = jnp.stack([dot(0, 0) + dot(1, 1), dot(0, 1) - dot(1, 0)]) * scale
    total = total.reshape(2, groups, bands // groups, bands).transpose(1, 0, 2, 3)
    total = total[jnp.arange(groups, dtype=jnp.int32) ^ me]
    return total[1::2], total[0::2]


def multiply(bras, kets, ket_of, bra_of, me, groups, scale):
    _, slots, part, bands = bras[0].shape
    rows = bands // groups
    depth = slots * part
    early = groups - 1
    near = pl.BlockSpec(memory_space=pltpu.VMEM)
    scalar = pl.BlockSpec(memory_space=pltpu.SMEM)

    def turned(chosen, d):
        first = chosen[0, d * slots : (d + 1) * slots].reshape(depth, bands).T
        second = chosen[1, d * slots : (d + 1) * slots].reshape(depth, bands).T
        upper = jnp.concatenate([first, second], axis=1)
        lower = jnp.concatenate([-second, first], axis=1)
        return jnp.concatenate([upper, lower], axis=0)

    def flat(ket_ref):
        return ket_ref[...].reshape(2 * depth, bands)

    def most(ket_of_ref, bra_of_ref, *refs):
        bra_refs, ket_refs = refs[:groups], refs[groups : groups + early]
        total_ref, last_ref, chosen = refs[groups + early :]
        for d in range(groups):

            def put(s, _, d=d):
                row = ket_of_ref[d * slots + s]
                row = jnp.where(row >= 0, row, groups * slots)
                for c in range(2):
                    chosen[c, row] = bra_refs[d][c, s]
                return 0

            lax.fori_loop(0, slots, put, 0, unroll=8)

        def clear(row, _):
            @pl.when(bra_of_ref[row] < 0)
            def _():
                for c in range(2):
                    chosen[c, row] = jnp.zeros((part, bands), jnp.bfloat16)

            return 0

        lax.fori_loop(0, groups * slots, clear, 0, unroll=8)
        for d in range(early):
            product = jnp.dot(turned(chosen, d), flat(ket_refs[d]), preferred_element_type=jnp.float32)
            if d == 0:
                total_ref[...] = product
            else:
                total_ref[...] += product
        last_ref[...] = turned(chosen, early)

    def rest(me_ref, total_ref, last_ref, ket_ref, give_ref, keep_ref, sums):
        sums[...] = total_ref[...] + jnp.dot(
            last_ref[...], flat(ket_ref), preferred_element_type=jnp.float32
        )
        for d in range(groups):
            out = give_ref if d % 2 else keep_ref
            start = (me_ref[0] ^ d) * rows
            for c in range(2):
                out[d // 2, c] = sums[pl.ds(pl.multiple_of(c * bands + start, rows), rows)] * scale

    flops = 8 * depth * bands * bands
    total, last = pl.pallas_call(
        most,
        in_specs=[scalar, scalar] + [near] * (groups + early),
        out_specs=[near, near],
        out_shape=[
            jax.ShapeDtypeStruct((2 * bands, bands), jnp.float32),
            jax.ShapeDtypeStruct((2 * bands, 2 * depth), jnp.bfloat16),
        ],
        scratch_shapes=[pltpu.VMEM((2, groups * slots + 1, part, bands), jnp.bfloat16)],
        compiler_params=pltpu.CompilerParams(vmem_limit_bytes=32 << 20),
        cost_estimate=pl.CostEstimate(flops=early * flops, bytes_accessed=1 << 20, transcendentals=0),
    )(ket_of, bra_of, *bras, *kets[:early])
    half = jax.ShapeDtypeStruct((groups // 2, 2, rows, bands), jnp.float32)
    return pl.pallas_call(
        rest,
        in_specs=[scalar, near, near, near],
        out_specs=[near, near],
        out_shape=[half, half],
        scratch_shapes=[pltpu.VMEM((2 * bands, bands), jnp.float32)],
        compiler_params=pltpu.CompilerParams(vmem_limit_bytes=16 << 20),
        cost_estimate=pl.CostEstimate(flops=flops, bytes_accessed=1 << 20, transcendentals=0),
    )(me.reshape(1), total, last, kets[early])


def local(coefficients, stick_count, dest_device, dest_slot, source_stick):
    groups = lax.axis_size("ga")
    me = lax.axis_index("ga").astype(jnp.int32)
    _, slots, _, bands, waves = coefficients.shape
    scale = (2 * groups * slots * waves) ** (-0.5)
    pieces = pack(coefficients[0], groups, me)
    mine = jnp.concatenate([stick_count, dest_device, dest_slot, source_stick], axis=1)[0]
    bra_info = gathered(mine, groups)
    ket_info = to_previous_pool(bra_info)
    bras, kets = [None] * groups, [None] * groups
    bras[0] = pieces[0]
    for d in [0, *range(1, groups // 2), *range(groups // 2, groups)]:
        if d:
            bras[d] = swapped_with(pieces[d], d)
            bras[d], previous = lax.optimization_barrier((bras[d], bras[d - 1]))
        kets[d] = to_previous_pool(bras[d])
    ket_of, bra_of = pair_lists(bra_info, ket_info, groups, slots, me)
    if (waves // groups) % 16:
        give, keep = multiply_plainly(bras, kets, ket_of, me, groups, scale)
    else:
        give, keep = multiply(bras, kets, ket_of, bra_of, me, groups, scale)
    distance = 1
    while True:
        keep = keep + swapped_with(give, distance)
        distance *= 2
        if distance == groups:
            break
        give, keep = keep[1::2], keep[0::2]
    return keep.reshape(1, 2, bands // groups, bands)


def solution(mesh):
    spec = P("pool", "ga")
    return jax.shard_map(
        local,
        mesh=mesh,
        in_specs=(P("pool", "ga", None, None, None), spec, spec, spec, spec),
        out_specs=P("pool", None, "ga", None),
        check_vma=False,
    )
```

profile of v0, /device:TPU:0, one launch (start us, length us, event | category | flops | bytes accessed | tf_op | source)
XLA Modules:
  0.0 170.7 jit_solution(8166293815284389761)
XLA Ops:
  0.1 2.2 %copy-done = bf16[1,32,2,256,128]{4,3,2,1,0:T(8,128)(2,1)S(1)} copy-done((bf16[1,32,2,256,128]{4,3,2,1,0:T(8,128)(2,1)S(1)}, bf16[1,32,2,256,128]{4,3,2,1,0:T(8,128)(2,1)}, u32[]{:S(2)}) %copy-start) | copy-done | bytes 4194328
  2.3 2.8 %shard_map.55 = (bf16[2,32,16,256]{3,2,1,0:T(8,128)(2,1)S(1)}, bf16[2,32,16,256]{3,2,1,0:T(8,128)(2,1)S(1)}, bf16[2,32,16,256]{3,2,1,0:T(8,128)(2,1)S(1)}, bf16[...) custom-call(bf16[128,128]{1,0:T(8,128)(2,1)S(1)} %fusion.select_ref,, ...), custom_call_target="tpu_custom_call" | custom-call | flops 536870912 | bytes 8388608 | tf_op jit(solution)/shard_map/pallas_call | solution.py:54
  5.1 3.0 %collective-permute-start.4 = (bf16[2,32,16,256]{3,2,1,0:T(8,128)(2,1)S(1)}, bf16[2,32,16,256]{3,2,1,0:T(8,128)(2,1)S(1)}, u32[]{:S(2)}, u32[]{:S(2)}) collective-permute-start(bf16[2,32,16,256]{3,2,1,0:T(8,128)(2,1)S(1)} %get-tuple-element.25), channel_id=1, source_target_pairs={{0,1},{1,0},{2,3},{3,2},{4,5},{5,4},{6,7},{7,6},{8,9},{9,8},{10,11... | collective-permute-start | bytes 1572872 | tf_op jit(solution)/shard_map/ppermute | solution.py:11
  8.1 1.6 collective-permute-start.5
  9.7 3.0 %collective-permute-start.7 = (bf16[2,32,16,256]{3,2,1,0:T(8,128)(2,1)S(1)}, bf16[2,32,16,256]{3,2,1,0:T(8,128)(2,1)S(1)}, u32[]{:S(2)}, u32[]{:S(2)}) collective-permute-start(bf16[2,32,16,256]{3,2,1,0:T(8,128)(2,1)S(1)} %get-tuple-element.31), channel_id=1, source_target_pairs={{0,4},{1,5},{2,6},{3,7},{4,0},{5,1},{6,2},{7,3},{8,12},{9,13},{10,... | collective-permute-start | bytes 1572872 | tf_op jit(solution)/shard_map/ppermute | solution.py:11
  12.7 1.3 collective-permute-start.8
  14.0 6.1 %collective-permute-done.4.refs_1_ = bf16[2,32,16,256]{3,2,1,0:T(8,128)(2,1)S(1)} collective-permute-done((bf16[2,32,16,256]{3,2,1,0:T(8,128)(2,1)S(1)}, bf16[2,32,16,256]{3,2,1,0:T(8,128)(2,1)S(1)}, u32[]{:S(2)}, u32[]{:S(2)}) %collective-permute-start.4) | collective-permute-done | bytes 524320 | tf_op jit(solution)/shard_map/ppermute | solution.py:11
  20.0 3.9 %collective-permute-start.9 = (bf16[2,32,16,256]{3,2,1,0:T(8,128)(2,1)S(1)}, bf16[2,32,16,256]{3,2,1,0:T(8,128)(2,1)S(1)}, u32[]{:S(2)}, u32[]{:S(2)}) collective-permute-start(bf16[2,32,16,256]{3,2,1,0:T(8,128)(2,1)S(1)} %get-tuple-element.35), channel_id=1, source_target_pairs={{0,6},{1,7},{2,4},{3,5},{4,2},{5,3},{6,0},{7,1},{8,14},{9,15},{10,... | collective-permute-start | bytes 1572872 | tf_op jit(solution)/shard_map/ppermute | solution.py:11
  24.5 19.9 %collective-permute-done.5.refs_2_ = bf16[2,32,16,256]{3,2,1,0:T(8,128)(2,1)S(1)} collective-permute-done((bf16[2,32,16,256]{3,2,1,0:T(8,128)(2,1)S(1)}, bf16[2,32,16,256]{3,2,1,0:T(8,128)(2,1)S(1)}, u32[]{:S(2)}, u32[]{:S(2)}) %collective-permute-start.5) | collective-permute-done | bytes 524320 | tf_op jit(solution)/shard_map/ppermute | solution.py:11
  44.5 9.0 %collective-permute-done.6.refs_3_ = bf16[2,32,16,256]{3,2,1,0:T(8,128)(2,1)S(1)} collective-permute-done((bf16[2,32,16,256]{3,2,1,0:T(8,128)(2,1)S(1)}, bf16[2,32,16,256]{3,2,1,0:T(8,128)(2,1)S(1)}, u32[]{:S(2)}, u32[]{:S(2)}) %collective-permute-start.6) | collective-permute-done | bytes 524320 | tf_op jit(solution)/shard_map/ppermute | solution.py:11
  53.4 3.8 %collective-permute-start.10 = (bf16[2,32,16,256]{3,2,1,0:T(8,128)(2,1)S(1)}, bf16[2,32,16,256]{3,2,1,0:T(8,128)(2,1)S(1)}, u32[]{:S(2)}, u32[]{:S(2)}) collective-permute-start(bf16[2,32,16,256]{3,2,1,0:T(8,128)(2,1)S(1)} %get-tuple-element.37), channel_id=1, source_target_pairs={{0,7},{1,6},{2,5},{3,4},{4,3},{5,2},{6,1},{7,0},{8,15},{9,14},{10,... | collective-permute-start | bytes 1572872 | tf_op jit(solution)/shard_map/ppermute | solution.py:11
  57.2 25.7 %collective-permute-done.8.refs_5_ = bf16[2,32,16,256]{3,2,1,0:T(8,128)(2,1)S(1)} collective-permute-done((bf16[2,32,16,256]{3,2,1,0:T(8,128)(2,1)S(1)}, bf16[2,32,16,256]{3,2,1,0:T(8,128)(2,1)S(1)}, u32[]{:S(2)}, u32[]{:S(2)}) %collective-permute-start.8) | collective-permute-done | bytes 524320 | tf_op jit(solution)/shard_map/ppermute | solution.py:11
  83.8 13.0 %collective-permute-start = (s32[1,97]{1,0:T(1,128)S(1)}, s32[1,97]{1,0:T(1,128)S(1)}, u32[]{:S(2)}, u32[]{:S(2)}) collective-permute-start(s32[1,97]{1,0:T(1,128)S(1)} %pad_add_fusion.3), channel_id=1, source_target_pairs={{0,4},{1,5},{2,6},{3,7},{4,0},{5,1},{6,2},{7,3},{8,12},{9,13},{10,... | collective-permute-start | bytes 1172 | tf_op jit(solution)/shard_map/ppermute | solution.py:11
  96.8 1.4 collective-permute-start.16
  98.2 4.3 %collective-permute-done = s32[1,97]{1,0:T(1,128)S(1)} collective-permute-done((s32[1,97]{1,0:T(1,128)S(1)}, s32[1,97]{1,0:T(1,128)S(1)}, u32[]{:S(2)}, u32[]{:S(2)}) %collective-permute-start) | collective-permute-done | bytes 420 | tf_op jit(solution)/shard_map/ppermute | solution.py:11
  103.4 2.7 %collective-permute-done.1 = s32[2,1,97]{2,1,0:T(1,128)S(1)} collective-permute-done((s32[2,1,97]{2,1,0:T(1,128)S(1)}, s32[2,1,97]{2,1,0:T(1,128)S(1)}, u32[]{:S(2)}, u32[]{:S(2)}) %collective-permute-start.1) | collective-permute-done | bytes 808 | tf_op jit(solution)/shard_map/ppermute | solution.py:11
  106.1 1.5 collective-permute-start.2
  107.6 2.0 %collective-permute-done.2 = s32[2,2,1,97]{3,0,2,1:T(2,128)S(1)} collective-permute-done((s32[2,2,1,97]{3,0,2,1:T(2,128)S(1)}, s32[2,2,1,97]{3,0,2,1:T(2,128)S(1)}, u32[]{:S(2)}, u32[]{:S(2)}) %collective-permute-start.2) | collective-permute-done | bytes 1584 | tf_op jit(solution)/shard_map/ppermute | solution.py:11
  109.8 1.3 collective-permute-done.3
  111.1 1.7 collective-permute-start.15
  113.7 1.6 collective-permute-start.13
  117.5 1.9 %collective-permute-done.15.refs_12_ = bf16[2,32,16,256]{3,2,1,0:T(8,128)(2,1)} collective-permute-done((bf16[2,32,16,256]{3,2,1,0:T(8,128)(2,1)S(1)}, bf16[2,32,16,256]{3,2,1,0:T(8,128)(2,1)}, u32[]{:S(2)}, u32[]{:S(2)}) %collective-permute-start.15) | collective-permute-done | bytes 524320 | tf_op jit(solution)/shard_map/ppermute | solution.py:16
  119.5 5.6 %collective-permute-done.14.refs_11_ = bf16[2,32,16,256]{3,2,1,0:T(8,128)(2,1)} collective-permute-done((bf16[2,32,16,256]{3,2,1,0:T(8,128)(2,1)S(1)}, bf16[2,32,16,256]{3,2,1,0:T(8,128)(2,1)}, u32[]{:S(2)}, u32[]{:S(2)}) %collective-permute-start.14) | collective-permute-done | bytes 524320 | tf_op jit(solution)/shard_map/ppermute | solution.py:16
  125.1 5.6 %collective-permute-done.13.refs_10_ = bf16[2,32,16,256]{3,2,1,0:T(8,128)(2,1)} collective-permute-done((bf16[2,32,16,256]{3,2,1,0:T(8,128)(2,1)S(1)}, bf16[2,32,16,256]{3,2,1,0:T(8,128)(2,1)}, u32[]{:S(2)}, u32[]{:S(2)}) %collective-permute-start.13) | collective-permute-done | bytes 524320 | tf_op jit(solution)/shard_map/ppermute | solution.py:16
  130.7 5.6 %collective-permute-done.12.refs_9_ = bf16[2,32,16,256]{3,2,1,0:T(8,128)(2,1)} collective-permute-done((bf16[2,32,16,256]{3,2,1,0:T(8,128)(2,1)S(1)}, bf16[2,32,16,256]{3,2,1,0:T(8,128)(2,1)}, u32[]{:S(2)}, u32[]{:S(2)}) %collective-permute-start.12) | collective-permute-done | bytes 524320 | tf_op jit(solution)/shard_map/ppermute | solution.py:16
  140.5 6.9 %shard_map.56 = (f32[512,256]{1,0:T(8,128)S(1)}, bf16[512,1024]{1,0:T(8,128)(2,1)S(1)}) custom-call(s32[256]{0:T(256)S(1)} %get-tuple-element.46.ket_of_ref, s32[256]{0:T(256)S(1)} %get-tuple-element.45.bra_of_ref, bf16[2,32,16,256]{3,2,1,0:T(8,128)(2,1)S(1)} %get-tuple-element.24.refs_0_, bf16[2,32,16,256]{3,2,1,0:T(8,128)(2,1)S(1)} %collective-permute-done.4.refs_1_, ...), custom_call_target="tpu_custom_call" | custom-call | flops 1879048192 | bytes 1048576 | tf_op jit(solution)/shard_map/pallas_call | solution.py:173
  147.4 1.5 shard_map.57
  148.9 1.6 collective-permute-start.19
  150.5 6.6 %collective-permute-done.19 = f32[4,2,32,256]{3,2,1,0:T(8,128)S(1)} collective-permute-done((f32[4,2,32,256]{3,2,1,0:T(8,128)S(1)}, f32[4,2,32,256]{3,2,1,0:T(8,128)S(1)}, u32[]{:S(2)}, u32[]{:S(2)}) %collective-permute-start.19) | collective-permute-done | bytes 262176 | tf_op jit(solution)/shard_map/ppermute | solution.py:11
  158.2 5.3 %collective-permute-done.20 = f32[2,2,32,256]{3,2,1,0:T(8,128)S(1)} collective-permute-done((f32[2,2,32,256]{3,2,1,0:T(8,128)S(1)}, f32[2,2,32,256]{3,2,1,0:T(8,128)S(1)}, u32[]{:S(2)}, u32[]{:S(2)}) %collective-permute-start.20) | collective-permute-done | bytes 131104 | tf_op jit(solution)/shard_map/ppermute | solution.py:11
  163.5 2.4 %collective-permute-start.21 = (f32[1,2,32,256]{3,2,1,0:T(8,128)S(1)}, f32[1,2,32,256]{3,2,1,0:T(8,128)S(1)}, u32[]{:S(2)}, u32[]{:S(2)}) collective-permute-start(f32[1,2,32,256]{3,2,1,0:T(8,128)S(1)} %slice.42), channel_id=1, source_target_pairs={{0,4},{1,5},{2,6},{3,7},{4,0},{5,1},{6,2},{7,3},{8,12},{9,13},{10,... | collective-permute-start | bytes 196616 | tf_op jit(solution)/shard_map/ppermute | solution.py:11
  165.9 4.2 %collective-permute-done.21 = f32[1,2,32,256]{3,2,1,0:T(8,128)S(1)} collective-permute-done((f32[1,2,32,256]{3,2,1,0:T(8,128)S(1)}, f32[1,2,32,256]{3,2,1,0:T(8,128)S(1)}, u32[]{:S(2)}, u32[]{:S(2)}) %collective-permute-start.21) | collective-permute-done | bytes 65568 | tf_op jit(solution)/shard_map/ppermute | solution.py:11
  (62 shorter events, 11.0 us)
Async XLA Ops:
  0.0 83.7 %copy-start.11 = (s32[1,32]{1,0:T(1,128)S(1)}, s32[1,32]{1,0:T(1,128)}, u32[]{:S(2)}) copy-start(s32[1,32]{1,0:T(1,128)} %param.7) | copy-start | bytes 388
  0.0 83.7 %copy-start.10 = (s32[1,32]{1,0:T(1,128)S(1)}, s32[1,32]{1,0:T(1,128)}, u32[]{:S(2)}) copy-start(s32[1,32]{1,0:T(1,128)} %param.8) | copy-start | bytes 388
  0.0 83.7 %copy-start.9 = (s32[1,32]{1,0:T(1,128)S(1)}, s32[1,32]{1,0:T(1,128)}, u32[]{:S(2)}) copy-start(s32[1,32]{1,0:T(1,128)} %param.9) | copy-start | bytes 388
  0.1 2.2 %copy-start = (bf16[1,32,2,256,128]{4,3,2,1,0:T(8,128)(2,1)S(1)}, bf16[1,32,2,256,128]{4,3,2,1,0:T(8,128)(2,1)}, u32[]{:S(2)}) copy-start(bf16[1,32,2,256,128]{4,3,2,1,0:T(8,128)(2,1)} %param.5) | copy-start | bytes 12582916
  5.1 15.0 %collective-permute-start.4 = (bf16[2,32,16,256]{3,2,1,0:T(8,128)(2,1)S(1)}, bf16[2,32,16,256]{3,2,1,0:T(8,128)(2,1)S(1)}, u32[]{:S(2)}, u32[]{:S(2)}) collective-permute-start(bf16[2,32,16,256]{3,2,1,0:T(8,128)(2,1)S(1)} %get-tuple-element.25), channel_id=1, source_target_pairs={{0,1},{1,0},{2,3},{3,2},{4,5},{5,4},{6,7},{7,6},{8,9},{9,8},{10,11... | collective-permute-start | bytes 1572872 | tf_op jit(solution)/shard_map/ppermute | solution.py:11
  8.1 36.3 %collective-permute-start.5 = (bf16[2,32,16,256]{3,2,1,0:T(8,128)(2,1)S(1)}, bf16[2,32,16,256]{3,2,1,0:T(8,128)(2,1)S(1)}, u32[]{:S(2)}, u32[]{:S(2)}) collective-permute-start(bf16[2,32,16,256]{3,2,1,0:T(8,128)(2,1)S(1)} %get-tuple-element.27), channel_id=1, source_target_pairs={{0,2},{1,3},{2,0},{3,1},{4,6},{5,7},{6,4},{7,5},{8,10},{9,11},{10,... | collective-permute-start | bytes 1572872 | tf_op jit(solution)/shard_map/ppermute | solution.py:11
  9.7 43.7 %collective-permute-start.6 = (bf16[2,32,16,256]{3,2,1,0:T(8,128)(2,1)S(1)}, bf16[2,32,16,256]{3,2,1,0:T(8,128)(2,1)S(1)}, u32[]{:S(2)}, u32[]{:S(2)}) collective-permute-start(bf16[2,32,16,256]{3,2,1,0:T(8,128)(2,1)S(1)} %get-tuple-element.29), channel_id=1, source_target_pairs={{0,3},{1,2},{2,1},{3,0},{4,7},{5,6},{6,5},{7,4},{8,11},{9,10},{10,... | collective-permute-start | bytes 1572872 | tf_op jit(solution)/shard_map/ppermute | solution.py:11
  9.7 47.5 %collective-permute-start.7 = (bf16[2,32,16,256]{3,2,1,0:T(8,128)(2,1)S(1)}, bf16[2,32,16,256]{3,2,1,0:T(8,128)(2,1)S(1)}, u32[]{:S(2)}, u32[]{:S(2)}) collective-permute-start(bf16[2,32,16,256]{3,2,1,0:T(8,128)(2,1)S(1)} %get-tuple-element.31), channel_id=1, source_target_pairs={{0,4},{1,5},{2,6},{3,7},{4,0},{5,1},{6,2},{7,3},{8,12},{9,13},{10,... | collective-permute-start | bytes 1572872 | tf_op jit(solution)/shard_map/ppermute | solution.py:11
  12.7 70.2 %collective-permute-start.8 = (bf16[2,32,16,256]{3,2,1,0:T(8,128)(2,1)S(1)}, bf16[2,32,16,256]{3,2,1,0:T(8,128)(2,1)S(1)}, u32[]{:S(2)}, u32[]{:S(2)}) collective-permute-start(bf16[2,32,16,256]{3,2,1,0:T(8,128)(2,1)S(1)} %get-tuple-element.33), channel_id=1, source_target_pairs={{0,5},{1,4},{2,7},{3,6},{4,1},{5,0},{6,3},{7,2},{8,13},{9,12},{10,... | collective-permute-start | bytes 1572872 | tf_op jit(solution)/shard_map/ppermute | solution.py:11
  20.0 62.9 %collective-permute-start.9 = (bf16[2,32,16,256]{3,2,1,0:T(8,128)(2,1)S(1)}, bf16[2,32,16,256]{3,2,1,0:T(8,128)(2,1)S(1)}, u32[]{:S(2)}, u32[]{:S(2)}) collective-permute-start(bf16[2,32,16,256]{3,2,1,0:T(8,128)(2,1)S(1)} %get-tuple-element.35), channel_id=1, source_target_pairs={{0,6},{1,7},{2,4},{3,5},{4,2},{5,3},{6,0},{7,1},{8,14},{9,15},{10,... | collective-permute-start | bytes 1572872 | tf_op jit(solution)/shard_map/ppermute | solution.py:11
  44.5 68.4 %collective-permute-start.11 = (bf16[2,32,16,256]{3,2,1,0:T(8,128)(2,1)S(1)}, bf16[2,32,16,256]{3,2,1,0:T(8,128)(2,1)S(1)}, u32[]{:S(2)}, u32[]{:S(2)}) collective-permute-start(bf16[2,32,16,256]{3,2,1,0:T(8,128)(2,1)S(1)} %get-tuple-element.24.refs_0_), channel_id=1, source_target_pairs={{0,24},{8,0},{16,8},{24,16},{1,25},{9,1},{17,9},{25,17},{2,26},{10... | collective-permute-start | bytes 1572872 | tf_op jit(solution)/shard_map/ppermute | solution.py:16
  53.4 59.3 %collective-permute-start.10 = (bf16[2,32,16,256]{3,2,1,0:T(8,128)(2,1)S(1)}, bf16[2,32,16,256]{3,2,1,0:T(8,128)(2,1)S(1)}, u32[]{:S(2)}, u32[]{:S(2)}) collective-permute-start(bf16[2,32,16,256]{3,2,1,0:T(8,128)(2,1)S(1)} %get-tuple-element.37), channel_id=1, source_target_pairs={{0,7},{1,6},{2,5},{3,4},{4,3},{5,2},{6,1},{7,0},{8,15},{9,14},{10,... | collective-permute-start | bytes 1572872 | tf_op jit(solution)/shard_map/ppermute | solution.py:11
  82.9 32.4 %collective-permute-start.17 = (bf16[2,32,16,256]{3,2,1,0:T(8,128)(2,1)S(1)}, bf16[2,32,16,256]{3,2,1,0:T(8,128)(2,1)S(1)}, u32[]{:S(2)}, u32[]{:S(2)}) collective-permute-start(bf16[2,32,16,256]{3,2,1,0:T(8,128)(2,1)S(1)} %collective-permute-done.9.refs_6_), channel_id=1, source_target_pairs={{0,24},{8,0},{16,8},{24,16},{1,25},{9,1},{17,9},{25,17},{2,26},{10... | collective-permute-start | bytes 1572872 | tf_op jit(solution)/shard_map/ppermute | solution.py:16
  83.8 18.7 %collective-permute-start = (s32[1,97]{1,0:T(1,128)S(1)}, s32[1,97]{1,0:T(1,128)S(1)}, u32[]{:S(2)}, u32[]{:S(2)}) collective-permute-start(s32[1,97]{1,0:T(1,128)S(1)} %pad_add_fusion.3), channel_id=1, source_target_pairs={{0,4},{1,5},{2,6},{3,7},{4,0},{5,1},{6,2},{7,3},{8,12},{9,13},{10,... | collective-permute-start | bytes 1172 | tf_op jit(solution)/shard_map/ppermute | solution.py:11
  96.8 19.7 %collective-permute-start.16 = (bf16[2,32,16,256]{3,2,1,0:T(8,128)(2,1)S(1)}, bf16[2,32,16,256]{3,2,1,0:T(8,128)(2,1)}, u32[]{:S(2)}, u32[]{:S(2)}) collective-permute-start(bf16[2,32,16,256]{3,2,1,0:T(8,128)(2,1)S(1)} %collective-permute-done.8.refs_5_), channel_id=1, source_target_pairs={{0,24},{8,0},{16,8},{24,16},{1,25},{9,1},{17,9},{25,17},{2,26},{10... | collective-permute-start | bytes 1572872 | tf_op jit(solution)/shard_map/ppermute | solution.py:16
  102.5 3.6 %collective-permute-start.1 = (s32[2,1,97]{2,1,0:T(1,128)S(1)}, s32[2,1,97]{2,1,0:T(1,128)S(1)}, u32[]{:S(2)}, u32[]{:S(2)}) collective-permute-start(s32[2,1,97]{2,1,0:T(1,128)S(1)} %pad_add_fusion.2), channel_id=1, source_target_pairs={{0,2},{1,3},{2,0},{3,1},{4,6},{5,7},{6,4},{7,5},{8,10},{9,11},{10,... | collective-permute-start | bytes 2336 | tf_op jit(solution)/shard_map/ppermute | solution.py:11
  106.1 3.6 %collective-permute-start.2 = (s32[2,2,1,97]{3,0,2,1:T(2,128)S(1)}, s32[2,2,1,97]{3,0,2,1:T(2,128)S(1)}, u32[]{:S(2)}, u32[]{:S(2)}) collective-permute-start(s32[2,2,1,97]{3,0,2,1:T(2,128)S(1)} %get-tuple-element.48), channel_id=1, source_target_pairs={{0,1},{1,0},{2,3},{3,2},{4,5},{5,4},{6,7},{7,6},{8,9},{9,8},{10,11... | collective-permute-start | bytes 4664 | tf_op jit(solution)/shard_map/ppermute | solution.py:11
  109.7 1.4 collective-permute-start.3
  111.1 8.4 %collective-permute-start.15 = (bf16[2,32,16,256]{3,2,1,0:T(8,128)(2,1)S(1)}, bf16[2,32,16,256]{3,2,1,0:T(8,128)(2,1)}, u32[]{:S(2)}, u32[]{:S(2)}) collective-permute-start(bf16[2,32,16,256]{3,2,1,0:T(8,128)(2,1)S(1)} %collective-permute-done.7.refs_4_), channel_id=1, source_target_pairs={{0,24},{8,0},{16,8},{24,16},{1,25},{9,1},{17,9},{25,17},{2,26},{10... | collective-permute-start | bytes 1572872 | tf_op jit(solution)/shard_map/ppermute | solution.py:16
  112.8 2.5 %copy-start.5 = (bf16[2,32,16,256]{3,2,1,0:T(8,128)(2,1)}, bf16[2,32,16,256]{3,2,1,0:T(8,128)(2,1)S(1)}, u32[]{:S(2)}) copy-start(bf16[2,32,16,256]{3,2,1,0:T(8,128)(2,1)S(1)} %collective-permute-done.10.refs_7_) | copy-start | bytes 1572868
  112.8 12.3 %collective-permute-start.14 = (bf16[2,32,16,256]{3,2,1,0:T(8,128)(2,1)S(1)}, bf16[2,32,16,256]{3,2,1,0:T(8,128)(2,1)}, u32[]{:S(2)}, u32[]{:S(2)}) collective-permute-start(bf16[2,32,16,256]{3,2,1,0:T(8,128)(2,1)S(1)} %collective-permute-done.6.refs_3_), channel_id=1, source_target_pairs={{0,24},{8,0},{16,8},{24,16},{1,25},{9,1},{17,9},{25,17},{2,26},{10... | collective-permute-start | bytes 1572872 | tf_op jit(solution)/shard_map/ppermute | solution.py:16
  112.8 0.9 copy-start.3
  113.7 17.0 %collective-permute-start.13 = (bf16[2,32,16,256]{3,2,1,0:T(8,128)(2,1)S(1)}, bf16[2,32,16,256]{3,2,1,0:T(8,128)(2,1)}, u32[]{:S(2)}, u32[]{:S(2)}) collective-permute-start(bf16[2,32,16,256]{3,2,1,0:T(8,128)(2,1)S(1)} %collective-permute-done.5.refs_2_), channel_id=1, source_target_pairs={{0,24},{8,0},{16,8},{24,16},{1,25},{9,1},{17,9},{25,17},{2,26},{10... | collective-permute-start | bytes 1572872 | tf_op jit(solution)/shard_map/ppermute | solution.py:16
  116.1 20.2 %collective-permute-start.12 = (bf16[2,32,16,256]{3,2,1,0:T(8,128)(2,1)S(1)}, bf16[2,32,16,256]{3,2,1,0:T(8,128)(2,1)}, u32[]{:S(2)}, u32[]{:S(2)}) collective-permute-start(bf16[2,32,16,256]{3,2,1,0:T(8,128)(2,1)S(1)} %collective-permute-done.4.refs_1_), channel_id=1, source_target_pairs={{0,24},{8,0},{16,8},{24,16},{1,25},{9,1},{17,9},{25,17},{2,26},{10... | collective-permute-start | bytes 1572872 | tf_op jit(solution)/shard_map/ppermute | solution.py:16
  116.5 30.9 %collective-permute-start.18 = (bf16[2,32,16,256]{3,2,1,0:T(8,128)(2,1)}, bf16[2,32,16,256]{3,2,1,0:T(8,128)(2,1)}, u32[]{:S(2)}, u32[]{:S(2)}) collective-permute-start(bf16[2,32,16,256]{3,2,1,0:T(8,128)(2,1)} %copy-done.5), channel_id=1, source_target_pairs={{0,24},{8,0},{16,8},{24,16},{1,25},{9,1},{17,9},{25,17},{2,26},{10... | collective-permute-start | bytes 1572872 | tf_op jit(solution)/shard_map/ppermute | solution.py:16
  136.3 1.0 copy-start.2
  137.4 1.0 copy-start.4
  138.4 1.0 copy-start.6
  139.4 1.0 copy-start.8
  148.9 8.3 %collective-permute-start.19 = (f32[4,2,32,256]{3,2,1,0:T(8,128)S(1)}, f32[4,2,32,256]{3,2,1,0:T(8,128)S(1)}, u32[]{:S(2)}, u32[]{:S(2)}) collective-permute-start(f32[4,2,32,256]{3,2,1,0:T(8,128)S(1)} %get-tuple-element.42), channel_id=1, source_target_pairs={{0,1},{1,0},{2,3},{3,2},{4,5},{5,4},{6,7},{7,6},{8,9},{9,8},{10,11... | collective-permute-start | bytes 786440 | tf_op jit(solution)/shard_map/ppermute | solution.py:11
  157.2 6.3 %collective-permute-start.20 = (f32[2,2,32,256]{3,2,1,0:T(8,128)S(1)}, f32[2,2,32,256]{3,2,1,0:T(8,128)S(1)}, u32[]{:S(2)}, u32[]{:S(2)}) collective-permute-start(f32[2,2,32,256]{3,2,1,0:T(8,128)S(1)} %slice.35), channel_id=1, source_target_pairs={{0,2},{1,3},{2,0},{3,1},{4,6},{5,7},{6,4},{7,5},{8,10},{9,11},{10,... | collective-permute-start | bytes 393224 | tf_op jit(solution)/shard_map/ppermute | solution.py:11
  163.5 6.6 %collective-permute-start.21 = (f32[1,2,32,256]{3,2,1,0:T(8,128)S(1)}, f32[1,2,32,256]{3,2,1,0:T(8,128)S(1)}, u32[]{:S(2)}, u32[]{:S(2)}) collective-permute-start(f32[1,2,32,256]{3,2,1,0:T(8,128)S(1)} %slice.42), channel_id=1, source_target_pairs={{0,4},{1,5},{2,6},{3,7},{4,0},{5,1},{6,2},{7,3},{8,12},{9,13},{10,... | collective-permute-start | bytes 196616 | tf_op jit(solution)/shard_map/ppermute | solution.py:11
  (2 other events, 1.6 us)
where the time goes:
time: 171 us
  waiting for transfers between devices  106 us (62%)
  starting transfers between devices  42.3 us (25%)
  Pallas kernels  11.1 us (6%)
  local copies, waits for them, and re-layouts  9.41 us (6%)
    ppermute x13, waiting for transfers between devices, swapped_with(): return lax.ppermute(value, 'ga', [(i, i ^ distance) for i in range(count)])  85.8 us
    ppermute x13, starting transfers between devices, swapped_with(): return lax.ppermute(value, 'ga', [(i, i ^ distance) for i in range(count)])  37 us
    ppermute x9, waiting for transfers between devices, to_previous_pool(): lax.ppermute(value, 'pool', [(i, (i - 1) % count) for i in range(count)])  20.1 us
    unnamed x24, local copies, waits for them, and re-layouts  8.81 us
    pallas_call x1, Pallas kernels, multiply(): pl.pallas_call(most, in_specs=[scalar, scalar] + [near] * (groups + early...  6.87 us
    ppermute x9, starting transfers between devices, to_previous_pool(): lax.ppermute(value, 'pool', [(i, (i - 1) % count) for i in range(count)])  5.32 us
  transfers between devices with their start and end apart: 22, of which 15 were waited for; matrix products, arithmetic and copies ran while one was open for 1% of the time, Pallas kernels for 4%

commit v1 on v0

--- a/solution.py
+++ b/solution.py
@@ -53,7 +53,7 @@
     near = pl.BlockSpec(memory_space=pltpu.VMEM)
     return pl.pallas_call(
         body,
-        in_specs=[near, pl.BlockSpec(memory_space=pl.ANY)],
+        in_specs=[near, pl.BlockSpec(memory_space=pltpu.HBM)],
         out_specs=[near] * groups,
         out_shape=[jax.ShapeDtypeStruct((2, slots, part, bands), jnp.bfloat16)] * groups,
         scratch_shapes=[
@@ -67,17 +67,11 @@
     )(select, x)
 
 
-def gathered(mine, groups):
-    rows = mine[None]
-    levels = []
-    distance = groups // 2
-    while distance:
-        other = swapped_with(rows, distance)
-        rows = jnp.stack([rows, other], axis=len(levels))
-        levels.append(2)
-        rows = rows.reshape(*levels, 1, mine.shape[0])
-        distance //= 2
-    return rows.reshape(groups, mine.shape[0])
+def passed_around(mine, groups):
+    rows = [mine]
+    for d in range(2, groups, 2):
+        rows.append(swapped_with(mine, d))
+    return rows
 
 
 def pair_lists(bra_info, ket_info, groups, slots, me):
@@ -194,6 +188,20 @@
     )(me.reshape(1), total, last, kets[early])
 
 
+def zero_like(value):
+    def body(_, out_ref):
+        out_ref[0, 0] = 0
+
+    scalar = pl.BlockSpec(memory_space=pltpu.SMEM)
+    return pl.pallas_call(
+        body,
+        in_specs=[scalar],
+        out_specs=scalar,
+        out_shape=jax.ShapeDtypeStruct((1, 1), jnp.int32),
+        compiler_params=pltpu.CompilerParams(vmem_limit_bytes=1 << 20),
+    )(value)
+
+
 def local(coefficients, stick_count, dest_device, dest_slot, source_stick):
     groups = lax.axis_size("ga")
     me = lax.axis_index("ga").astype(jnp.int32)
@@ -201,16 +209,26 @@
     scale = (2 * groups * slots * waves) ** (-0.5)
     pieces = pack(coefficients[0], groups, me)
     mine = jnp.concatenate([stick_count, dest_device, dest_slot, source_stick], axis=1)[0]
-    bra_info = gathered(mine, groups)
-    ket_info = to_previous_pool(bra_info)
+    info = passed_around(mine, groups)
     bras, kets = [None] * groups, [None] * groups
     bras[0] = pieces[0]
-    for d in [0, *range(1, groups // 2), *range(groups // 2, groups)]:
-        if d:
-            bras[d] = swapped_with(pieces[d], d)
-            bras[d], previous = lax.optimization_barrier((bras[d], bras[d - 1]))
+    arrivals = interleaved(range(1, groups // 2), range(groups // 2, groups))
+    kets[0] = to_previous_pool(bras[0])
+    anchor = me.reshape(1, 1)
+    for place, d in enumerate(arrivals):
+        bras[d] = swapped_with(pieces[d], d)
         kets[d] = to_previous_pool(bras[d])
-    ket_of, bra_of = pair_lists(bra_info, ket_info, groups, slots, me)
+        if place == len(arrivals) - 1:
+            break
+        anchor = zero_like(anchor)
+        if place == len(arrivals) - 2:
+            before_last = anchor
+        if place == groups // 2:
+            even = jnp.stack(info) + anchor
+    odd = swapped_with(even, 1)
+    bra_info = jnp.stack([even, odd], axis=1).reshape(groups, mine.shape[0])
+    ket_info = to_previous_pool(bra_info)
+    ket_of, bra_of = pair_lists(bra_info, ket_info + before_last, groups, slots, me)
     if (waves // groups) % 16:
         give, keep = multiply_plainly(bras, kets, ket_of, me, groups, scale)
     else:
@@ -225,6 +243,12 @@
     return keep.reshape(1, 2, bands // groups, bands)
 
 
+def interleaved(first, second):
+    first, second = list(first), list(second)
+    mixed = [item for pair in zip(first, second) for item in pair]
+    return mixed + second[len(first) :]
+
+
 def solution(mesh):
     spec = P("pool", "ga")
     return jax.shard_map(

time: 171 us -> 163 us (0.953)
  the two profiles are of different devices: /device:TPU:0 before, /device:TPU:1 now
where the time goes in v1:
time: 163 us
  waiting for transfers between devices  96.8 us (59%)
  starting transfers between devices  39.5 us (24%)
  Pallas kernels  18.9 us (12%)
  other arithmetic  3.74 us (2%)
  local copies, waits for them, and re-layouts  2.75 us (2%)
    ppermute x14, waiting for transfers between devices, swapped_with(): return lax.ppermute(value, 'ga', [(i, i ^ distance) for i in range(count)])  67.9 us
    ppermute x14, starting transfers between devices, swapped_with(): return lax.ppermute(value, 'ga', [(i, i ^ distance) for i in range(count)])  31.1 us
    ppermute x9, waiting for transfers between devices, to_previous_pool(): lax.ppermute(value, 'pool', [(i, (i - 1) % count) for i in range(count)])  28.9 us
    ppermute x9, starting transfers between devices, to_previous_pool(): lax.ppermute(value, 'pool', [(i, (i - 1) % count) for i in range(count)])  8.44 us
    pallas_call x1, Pallas kernels, multiply(): pl.pallas_call(most, in_specs=[scalar, scalar] + [near] * (groups + early...  7.51 us
    pallas_call x6, Pallas kernels, zero_like(): pl.pallas_call(body, in_specs=[scalar], out_specs=scalar, out_shape=jax.S...  6.08 us
    pallas_call x1, Pallas kernels, pack(): pl.pallas_call(body, in_specs=[near, pl.BlockSpec(memory_space=pltpu.HBM)...  3.74 us
  transfers between devices with their start and end apart: 23, of which 13 were waited for; matrix products, arithmetic and copies ran while one was open for 2% of the time, Pallas kernels for 11%

profile of v1, /device:TPU:1, one launch (start us, length us, event | category | flops | bytes accessed | tf_op | source)
XLA Modules:
  0.0 162.6 jit_solution(6581989077100288344)
XLA Ops:
  1.5 2.1 %collective-permute-start = (s32[97]{0:T(128)S(1)}, s32[97]{0:T(128)S(1)}, u32[]{:S(2)}, u32[]{:S(2)}) collective-permute-start(s32[97]{0:T(128)S(1)} %bitcast.20), channel_id=1, source_target_pairs={{0,2},{1,3},{2,0},{3,1},{4,6},{5,7},{6,4},{7,5},{8,10},{9,11},{10,... | collective-permute-start | bytes 1172 | tf_op jit(solution)/shard_map/ppermute | solution.py:11
  3.6 2.3 %collective-permute-start.1 = (s32[97]{0:T(128)S(1)}, s32[97]{0:T(128)S(1)}, u32[]{:S(2)}, u32[]{:S(2)}) collective-permute-start(s32[97]{0:T(128)S(1)} %bitcast.21), channel_id=1, source_target_pairs={{0,4},{1,5},{2,6},{3,7},{4,0},{5,1},{6,2},{7,3},{8,12},{9,13},{10,... | collective-permute-start | bytes 1172 | tf_op jit(solution)/shard_map/ppermute | solution.py:11
  6.0 2.2 %copy-done = bf16[1,32,2,256,128]{4,3,2,1,0:T(8,128)(2,1)S(1)} copy-done((bf16[1,32,2,256,128]{4,3,2,1,0:T(8,128)(2,1)S(1)}, bf16[1,32,2,256,128]{4,3,2,1,0:T(8,128)(2,1)}, u32[]{:S(2)}) %copy-start) | copy-done | bytes 4194328
  8.2 3.7 %shard_map.61 = (bf16[2,32,16,256]{3,2,1,0:T(8,128)(2,1)S(1)}, bf16[2,32,16,256]{3,2,1,0:T(8,128)(2,1)S(1)}, bf16[2,32,16,256]{3,2,1,0:T(8,128)(2,1)S(1)}, bf16[...) custom-call(bf16[128,128]{1,0:T(8,128)(2,1)S(1)} %fusion.select_ref,, ...), custom_call_target="tpu_custom_call" | custom-call | flops 536870912 | bytes 8388608 | tf_op jit(solution)/shard_map/pallas_call | solution.py:54
  11.9 1.3 collective-permute-start.5
  14.1 1.1 shard_map.56._
  16.3 1.1 shard_map.58._
  18.5 1.2 collective-permute-start.7
  19.7 2.2 %collective-permute-start.8 = (bf16[2,32,16,256]{3,2,1,0:T(8,128)(2,1)S(1)}, bf16[2,32,16,256]{3,2,1,0:T(8,128)(2,1)S(1)}, u32[]{:S(2)}, u32[]{:S(2)}) collective-permute-start(bf16[2,32,16,256]{3,2,1,0:T(8,128)(2,1)S(1)} %get-tuple-element.21), channel_id=1, source_target_pairs={{0,4},{1,5},{2,6},{3,7},{4,0},{5,1},{6,2},{7,3},{8,12},{9,13},{10,... | collective-permute-start | bytes 1572872 | tf_op jit(solution)/shard_map/ppermute | solution.py:11
  22.6 1.1 collective-permute-start.3
  25.4 3.2 %collective-permute-start.4 = (s32[8,97]{1,0:T(8,128)S(1)}, s32[8,97]{1,0:T(8,128)S(1)}, u32[]{:S(2)}, u32[]{:S(2)}) collective-permute-start(s32[8,97]{1,0:T(8,128)S(1)} %bitcast.18), channel_id=1, source_target_pairs={{0,24},{8,0},{16,8},{24,16},{1,25},{9,1},{17,9},{25,17},{2,26},{10... | collective-permute-start | bytes 9320 | tf_op jit(solution)/shard_map/ppermute | solution.py:16
  28.6 2.7 %collective-permute-done.4 = s32[8,97]{1,0:T(8,128)S(1)} collective-permute-done((s32[8,97]{1,0:T(8,128)S(1)}, s32[8,97]{1,0:T(8,128)S(1)}, u32[]{:S(2)}, u32[]{:S(2)}) %collective-permute-start.4) | collective-permute-done | bytes 3136 | tf_op jit(solution)/shard_map/ppermute | solution.py:16
  31.3 1.3 collective-permute-start.9
  32.7 3.5 %collective-permute-start.10 = (bf16[2,32,16,256]{3,2,1,0:T(8,128)(2,1)}, bf16[2,32,16,256]{3,2,1,0:T(8,128)(2,1)}, u32[]{:S(2)}, u32[]{:S(2)}) collective-permute-start(bf16[2,32,16,256]{3,2,1,0:T(8,128)(2,1)} %get-tuple-element.23), channel_id=1, source_target_pairs={{0,6},{1,7},{2,4},{3,5},{4,2},{5,3},{6,0},{7,1},{8,14},{9,15},{10,... | collective-permute-start | bytes 1572872 | tf_op jit(solution)/shard_map/ppermute | solution.py:11
  36.2 4.7 %collective-permute-done.6.refs_2_ = bf16[2,32,16,256]{3,2,1,0:T(8,128)(2,1)S(1)} collective-permute-done((bf16[2,32,16,256]{3,2,1,0:T(8,128)(2,1)S(1)}, bf16[2,32,16,256]{3,2,1,0:T(8,128)(2,1)S(1)}, u32[]{:S(2)}, u32[]{:S(2)}) %collective-permute-start.6) | collective-permute-done | bytes 524320 | tf_op jit(solution)/shard_map/ppermute | solution.py:11
  40.9 11.4 %collective-permute-done.7.refs_3_ = bf16[2,32,16,256]{3,2,1,0:T(8,128)(2,1)S(1)} collective-permute-done((bf16[2,32,16,256]{3,2,1,0:T(8,128)(2,1)S(1)}, bf16[2,32,16,256]{3,2,1,0:T(8,128)(2,1)S(1)}, u32[]{:S(2)}, u32[]{:S(2)}) %collective-permute-start.7) | collective-permute-done | bytes 524320 | tf_op jit(solution)/shard_map/ppermute | solution.py:11
  52.3 2.4 %collective-permute-start.12 = (bf16[2,32,16,256]{3,2,1,0:T(8,128)(2,1)S(1)}, bf16[2,32,16,256]{3,2,1,0:T(8,128)(2,1)}, u32[]{:S(2)}, u32[]{:S(2)}) collective-permute-start(bf16[2,32,16,256]{3,2,1,0:T(8,128)(2,1)S(1)} %get-tuple-element.17.refs_0_), channel_id=1, source_target_pairs={{0,24},{8,0},{16,8},{24,16},{1,25},{9,1},{17,9},{25,17},{2,26},{10... | collective-permute-start | bytes 1572872 | tf_op jit(solution)/shard_map/ppermute | solution.py:16
  54.7 37.0 %collective-permute-done.9.refs_5_ = bf16[2,32,16,256]{3,2,1,0:T(8,128)(2,1)S(1)} collective-permute-done((bf16[2,32,16,256]{3,2,1,0:T(8,128)(2,1)S(1)}, bf16[2,32,16,256]{3,2,1,0:T(8,128)(2,1)S(1)}, u32[]{:S(2)}, u32[]{:S(2)}) %collective-permute-start.9) | collective-permute-done | bytes 524320 | tf_op jit(solution)/shard_map/ppermute | solution.py:11
  91.8 1.1 shard_map.60
  94.0 1.8 %collective-permute-start.16 = (bf16[2,32,16,256]{3,2,1,0:T(8,128)(2,1)S(1)}, bf16[2,32,16,256]{3,2,1,0:T(8,128)(2,1)}, u32[]{:S(2)}, u32[]{:S(2)}) collective-permute-start(bf16[2,32,16,256]{3,2,1,0:T(8,128)(2,1)S(1)} %collective-permute-done.8.refs_4_), channel_id=1, source_target_pairs={{0,24},{8,0},{16,8},{24,16},{1,25},{9,1},{17,9},{25,17},{2,26},{10... | collective-permute-start | bytes 1572872 | tf_op jit(solution)/shard_map/ppermute | solution.py:16
  96.0 4.9 %collective-permute-done.14.refs_10_ = bf16[2,32,16,256]{3,2,1,0:T(8,128)(2,1)} collective-permute-done((bf16[2,32,16,256]{3,2,1,0:T(8,128)(2,1)S(1)}, bf16[2,32,16,256]{3,2,1,0:T(8,128)(2,1)}, u32[]{:S(2)}, u32[]{:S(2)}) %collective-permute-start.14) | collective-permute-done | bytes 524320 | tf_op jit(solution)/shard_map/ppermute | solution.py:16
  102.1 4.4 %collective-permute-done.15.refs_11_ = bf16[2,32,16,256]{3,2,1,0:T(8,128)(2,1)} collective-permute-done((bf16[2,32,16,256]{3,2,1,0:T(8,128)(2,1)S(1)}, bf16[2,32,16,256]{3,2,1,0:T(8,128)(2,1)}, u32[]{:S(2)}, u32[]{:S(2)}) %collective-permute-start.15) | collective-permute-done | bytes 524320 | tf_op jit(solution)/shard_map/ppermute | solution.py:16
  106.5 5.6 %collective-permute-done.16.refs_12_ = bf16[2,32,16,256]{3,2,1,0:T(8,128)(2,1)} collective-permute-done((bf16[2,32,16,256]{3,2,1,0:T(8,128)(2,1)S(1)}, bf16[2,32,16,256]{3,2,1,0:T(8,128)(2,1)}, u32[]{:S(2)}, u32[]{:S(2)}) %collective-permute-start.16) | collective-permute-done | bytes 524320 | tf_op jit(solution)/shard_map/ppermute | solution.py:16
  112.1 5.6 %collective-permute-done.17.refs_13_ = bf16[2,32,16,256]{3,2,1,0:T(8,128)(2,1)} collective-permute-done((bf16[2,32,16,256]{3,2,1,0:T(8,128)(2,1)S(1)}, bf16[2,32,16,256]{3,2,1,0:T(8,128)(2,1)}, u32[]{:S(2)}, u32[]{:S(2)}) %collective-permute-start.17) | collective-permute-done | bytes 524320 | tf_op jit(solution)/shard_map/ppermute | solution.py:16
  117.7 5.6 %collective-permute-done.18.refs_14_ = bf16[2,32,16,256]{3,2,1,0:T(8,128)(2,1)} collective-permute-done((bf16[2,32,16,256]{3,2,1,0:T(8,128)(2,1)}, bf16[2,32,16,256]{3,2,1,0:T(8,128)(2,1)}, u32[]{:S(2)}, u32[]{:S(2)}) %collective-permute-start.18) | collective-permute-done | bytes 524320 | tf_op jit(solution)/shard_map/ppermute | solution.py:16
  123.3 7.5 %shard_map.62 = (f32[512,256]{1,0:T(8,128)S(1)}, bf16[512,1024]{1,0:T(8,128)(2,1)S(1)}) custom-call(s32[256]{0:T(256)S(1)} %get-tuple-element.32.ket_of_ref, s32[256]{0:T(256)S(1)} %get-tuple-element.31.bra_of_ref, bf16[2,32,16,256]{3,2,1,0:T(8,128)(2,1)S(1)} %get-tuple-element.17.refs_0_, bf16[2,32,16,256]{3,2,1,0:T(8,128)(2,1)S(1)} %collective-permute-done.5.refs_1_, ...), custom_call_target="tpu_custom_call" | custom-call | flops 1879048192 | bytes 1048576 | tf_op jit(solution)/shard_map/pallas_call | solution.py:167
  130.9 1.5 shard_map.63
  133.1 6.4 %collective-permute-done.20 = f32[4,2,32,256]{3,2,1,0:T(8,128)S(1)} collective-permute-done((f32[4,2,32,256]{3,2,1,0:T(8,128)S(1)}, f32[4,2,32,256]{3,2,1,0:T(8,128)S(1)}, u32[]{:S(2)}, u32[]{:S(2)}) %collective-permute-start.20) | collective-permute-done | bytes 262176 | tf_op jit(solution)/shard_map/ppermute | solution.py:11
  139.6 11.7 %collective-permute-start.21 = (f32[2,2,32,256]{3,2,1,0:T(8,128)S(1)}, f32[2,2,32,256]{3,2,1,0:T(8,128)S(1)}, u32[]{:S(2)}, u32[]{:S(2)}) collective-permute-start(f32[2,2,32,256]{3,2,1,0:T(8,128)S(1)} %slice.35), channel_id=1, source_target_pairs={{0,2},{1,3},{2,0},{3,1},{4,6},{5,7},{6,4},{7,5},{8,10},{9,11},{10,... | collective-permute-start | bytes 393224 | tf_op jit(solution)/shard_map/ppermute | solution.py:11
  151.3 3.5 %collective-permute-done.21 = f32[2,2,32,256]{3,2,1,0:T(8,128)S(1)} collective-permute-done((f32[2,2,32,256]{3,2,1,0:T(8,128)S(1)}, f32[2,2,32,256]{3,2,1,0:T(8,128)S(1)}, u32[]{:S(2)}, u32[]{:S(2)}) %collective-permute-start.21) | collective-permute-done | bytes 131104 | tf_op jit(solution)/shard_map/ppermute | solution.py:11
  154.8 3.3 %collective-permute-start.22 = (f32[1,2,32,256]{3,2,1,0:T(8,128)S(1)}, f32[1,2,32,256]{3,2,1,0:T(8,128)S(1)}, u32[]{:S(2)}, u32[]{:S(2)}) collective-permute-start(f32[1,2,32,256]{3,2,1,0:T(8,128)S(1)} %slice.42), channel_id=1, source_target_pairs={{0,4},{1,5},{2,6},{3,7},{4,0},{5,1},{6,2},{7,3},{8,12},{9,13},{10,... | collective-permute-start | bytes 196616 | tf_op jit(solution)/shard_map/ppermute | solution.py:11
  158.1 3.9 %collective-permute-done.22 = f32[1,2,32,256]{3,2,1,0:T(8,128)S(1)} collective-permute-done((f32[1,2,32,256]{3,2,1,0:T(8,128)S(1)}, f32[1,2,32,256]{3,2,1,0:T(8,128)S(1)}, u32[]{:S(2)}, u32[]{:S(2)}) %collective-permute-start.22) | collective-permute-done | bytes 65568 | tf_op jit(solution)/shard_map/ppermute | solution.py:11
  (54 shorter events, 10.2 us)
Async XLA Ops:
  0.0 21.9 %copy-start.3 = (s32[1,32]{1,0:T(1,128)S(1)}, s32[1,32]{1,0:T(1,128)}, u32[]{:S(2)}) copy-start(s32[1,32]{1,0:T(1,128)} %param.7) | copy-start | bytes 388
  0.0 21.9 %copy-start.2 = (s32[1,32]{1,0:T(1,128)S(1)}, s32[1,32]{1,0:T(1,128)}, u32[]{:S(2)}) copy-start(s32[1,32]{1,0:T(1,128)} %param.8) | copy-start | bytes 388
  0.0 21.9 %copy-start.1 = (s32[1,32]{1,0:T(1,128)S(1)}, s32[1,32]{1,0:T(1,128)}, u32[]{:S(2)}) copy-start(s32[1,32]{1,0:T(1,128)} %param.9) | copy-start | bytes 388
  1.5 17.1 %collective-permute-start = (s32[97]{0:T(128)S(1)}, s32[97]{0:T(128)S(1)}, u32[]{:S(2)}, u32[]{:S(2)}) collective-permute-start(s32[97]{0:T(128)S(1)} %bitcast.20), channel_id=1, source_target_pairs={{0,2},{1,3},{2,0},{3,1},{4,6},{5,7},{6,4},{7,5},{8,10},{9,11},{10,... | collective-permute-start | bytes 1172 | tf_op jit(solution)/shard_map/ppermute | solution.py:11
  3.6 16.1 %collective-permute-start.1 = (s32[97]{0:T(128)S(1)}, s32[97]{0:T(128)S(1)}, u32[]{:S(2)}, u32[]{:S(2)}) collective-permute-start(s32[97]{0:T(128)S(1)} %bitcast.21), channel_id=1, source_target_pairs={{0,4},{1,5},{2,6},{3,7},{4,0},{5,1},{6,2},{7,3},{8,12},{9,13},{10,... | collective-permute-start | bytes 1172 | tf_op jit(solution)/shard_map/ppermute | solution.py:11
  5.9 16.0 %collective-permute-start.2 = (s32[97]{0:T(128)S(1)}, s32[97]{0:T(128)S(1)}, u32[]{:S(2)}, u32[]{:S(2)}) collective-permute-start(s32[97]{0:T(128)S(1)} %bitcast.22), channel_id=1, source_target_pairs={{0,6},{1,7},{2,4},{3,5},{4,2},{5,3},{6,0},{7,1},{8,14},{9,15},{10,... | collective-permute-start | bytes 1172 | tf_op jit(solution)/shard_map/ppermute | solution.py:11
  6.0 2.2 %copy-start = (bf16[1,32,2,256,128]{4,3,2,1,0:T(8,128)(2,1)S(1)}, bf16[1,32,2,256,128]{4,3,2,1,0:T(8,128)(2,1)}, u32[]{:S(2)}) copy-start(bf16[1,32,2,256,128]{4,3,2,1,0:T(8,128)(2,1)} %param.5) | copy-start | bytes 12582916
  11.9 20.8 %collective-permute-start.5 = (bf16[2,32,16,256]{3,2,1,0:T(8,128)(2,1)S(1)}, bf16[2,32,16,256]{3,2,1,0:T(8,128)(2,1)S(1)}, u32[]{:S(2)}, u32[]{:S(2)}) collective-permute-start(bf16[2,32,16,256]{3,2,1,0:T(8,128)(2,1)S(1)} %get-tuple-element.18), channel_id=1, source_target_pairs={{0,1},{1,0},{2,3},{3,2},{4,5},{5,4},{6,7},{7,6},{8,9},{9,8},{10,11... | collective-permute-start | bytes 1572872 | tf_op jit(solution)/shard_map/ppermute | solution.py:11
  13.2 27.7 %collective-permute-start.6 = (bf16[2,32,16,256]{3,2,1,0:T(8,128)(2,1)S(1)}, bf16[2,32,16,256]{3,2,1,0:T(8,128)(2,1)S(1)}, u32[]{:S(2)}, u32[]{:S(2)}) collective-permute-start(bf16[2,32,16,256]{3,2,1,0:T(8,128)(2,1)S(1)} %get-tuple-element.19), channel_id=1, source_target_pairs={{0,2},{1,3},{2,0},{3,1},{4,6},{5,7},{6,4},{7,5},{8,10},{9,11},{10,... | collective-permute-start | bytes 1572872 | tf_op jit(solution)/shard_map/ppermute | solution.py:11
  18.5 33.8 %collective-permute-start.7 = (bf16[2,32,16,256]{3,2,1,0:T(8,128)(2,1)S(1)}, bf16[2,32,16,256]{3,2,1,0:T(8,128)(2,1)S(1)}, u32[]{:S(2)}, u32[]{:S(2)}) collective-permute-start(bf16[2,32,16,256]{3,2,1,0:T(8,128)(2,1)S(1)} %get-tuple-element.20), channel_id=1, source_target_pairs={{0,3},{1,2},{2,1},{3,0},{4,7},{5,6},{6,5},{7,4},{8,11},{9,10},{10,... | collective-permute-start | bytes 1572872 | tf_op jit(solution)/shard_map/ppermute | solution.py:11
  19.7 35.0 %collective-permute-start.8 = (bf16[2,32,16,256]{3,2,1,0:T(8,128)(2,1)S(1)}, bf16[2,32,16,256]{3,2,1,0:T(8,128)(2,1)S(1)}, u32[]{:S(2)}, u32[]{:S(2)}) collective-permute-start(bf16[2,32,16,256]{3,2,1,0:T(8,128)(2,1)S(1)} %get-tuple-element.21), channel_id=1, source_target_pairs={{0,4},{1,5},{2,6},{3,7},{4,0},{5,1},{6,2},{7,3},{8,12},{9,13},{10,... | collective-permute-start | bytes 1572872 | tf_op jit(solution)/shard_map/ppermute | solution.py:11
  22.6 2.8 %collective-permute-start.3 = (s32[4,97]{1,0:T(4,128)S(1)}, s32[4,97]{1,0:T(4,128)S(1)}, u32[]{:S(2)}, u32[]{:S(2)}) collective-permute-start(s32[4,97]{1,0:T(4,128)S(1)} %add_add_fusion.1), channel_id=1, source_target_pairs={{0,1},{1,0},{2,3},{3,2},{4,5},{5,4},{6,7},{7,6},{8,9},{9,8},{10,11... | collective-permute-start | bytes 4664 | tf_op jit(solution)/shard_map/ppermute | solution.py:11
  25.4 6.0 %collective-permute-start.4 = (s32[8,97]{1,0:T(8,128)S(1)}, s32[8,97]{1,0:T(8,128)S(1)}, u32[]{:S(2)}, u32[]{:S(2)}) collective-permute-start(s32[8,97]{1,0:T(8,128)S(1)} %bitcast.18), channel_id=1, source_target_pairs={{0,24},{8,0},{16,8},{24,16},{1,25},{9,1},{17,9},{25,17},{2,26},{10... | collective-permute-start | bytes 9320 | tf_op jit(solution)/shard_map/ppermute | solution.py:16
  31.3 60.4 %collective-permute-start.9 = (bf16[2,32,16,256]{3,2,1,0:T(8,128)(2,1)S(1)}, bf16[2,32,16,256]{3,2,1,0:T(8,128)(2,1)S(1)}, u32[]{:S(2)}, u32[]{:S(2)}) collective-permute-start(bf16[2,32,16,256]{3,2,1,0:T(8,128)(2,1)S(1)} %get-tuple-element.22), channel_id=1, source_target_pairs={{0,5},{1,4},{2,7},{3,6},{4,1},{5,0},{6,3},{7,2},{8,13},{9,12},{10,... | collective-permute-start | bytes 1572872 | tf_op jit(solution)/shard_map/ppermute | solution.py:11
  32.7 60.5 %collective-permute-start.10 = (bf16[2,32,16,256]{3,2,1,0:T(8,128)(2,1)}, bf16[2,32,16,256]{3,2,1,0:T(8,128)(2,1)}, u32[]{:S(2)}, u32[]{:S(2)}) collective-permute-start(bf16[2,32,16,256]{3,2,1,0:T(8,128)(2,1)} %get-tuple-element.23), channel_id=1, source_target_pairs={{0,6},{1,7},{2,4},{3,5},{4,2},{5,3},{6,0},{7,1},{8,14},{9,15},{10,... | collective-permute-start | bytes 1572872 | tf_op jit(solution)/shard_map/ppermute | solution.py:11
  40.9 53.2 %collective-permute-start.11 = (bf16[2,32,16,256]{3,2,1,0:T(8,128)(2,1)}, bf16[2,32,16,256]{3,2,1,0:T(8,128)(2,1)}, u32[]{:S(2)}, u32[]{:S(2)}) collective-permute-start(bf16[2,32,16,256]{3,2,1,0:T(8,128)(2,1)} %get-tuple-element.24), channel_id=1, source_target_pairs={{0,7},{1,6},{2,5},{3,4},{4,3},{5,2},{6,1},{7,0},{8,15},{9,14},{10,... | collective-permute-start | bytes 1572872 | tf_op jit(solution)/shard_map/ppermute | solution.py:11
  52.3 43.5 %collective-permute-start.12 = (bf16[2,32,16,256]{3,2,1,0:T(8,128)(2,1)S(1)}, bf16[2,32,16,256]{3,2,1,0:T(8,128)(2,1)}, u32[]{:S(2)}, u32[]{:S(2)}) collective-permute-start(bf16[2,32,16,256]{3,2,1,0:T(8,128)(2,1)S(1)} %get-tuple-element.17.refs_0_), channel_id=1, source_target_pairs={{0,24},{8,0},{16,8},{24,16},{1,25},{9,1},{17,9},{25,17},{2,26},{10... | collective-permute-start | bytes 1572872 | tf_op jit(solution)/shard_map/ppermute | solution.py:16
  54.7 41.2 %collective-permute-start.13 = (bf16[2,32,16,256]{3,2,1,0:T(8,128)(2,1)S(1)}, bf16[2,32,16,256]{3,2,1,0:T(8,128)(2,1)}, u32[]{:S(2)}, u32[]{:S(2)}) collective-permute-start(bf16[2,32,16,256]{3,2,1,0:T(8,128)(2,1)S(1)} %collective-permute-done.5.refs_1_), channel_id=1, source_target_pairs={{0,24},{8,0},{16,8},{24,16},{1,25},{9,1},{17,9},{25,17},{2,26},{10... | collective-permute-start | bytes 1572872 | tf_op jit(solution)/shard_map/ppermute | solution.py:16
  91.7 9.1 %collective-permute-start.14 = (bf16[2,32,16,256]{3,2,1,0:T(8,128)(2,1)S(1)}, bf16[2,32,16,256]{3,2,1,0:T(8,128)(2,1)}, u32[]{:S(2)}, u32[]{:S(2)}) collective-permute-start(bf16[2,32,16,256]{3,2,1,0:T(8,128)(2,1)S(1)} %collective-permute-done.6.refs_2_), channel_id=1, source_target_pairs={{0,24},{8,0},{16,8},{24,16},{1,25},{9,1},{17,9},{25,17},{2,26},{10... | collective-permute-start | bytes 1572872 | tf_op jit(solution)/shard_map/ppermute | solution.py:16
  93.2 13.3 %collective-permute-start.15 = (bf16[2,32,16,256]{3,2,1,0:T(8,128)(2,1)S(1)}, bf16[2,32,16,256]{3,2,1,0:T(8,128)(2,1)}, u32[]{:S(2)}, u32[]{:S(2)}) collective-permute-start(bf16[2,32,16,256]{3,2,1,0:T(8,128)(2,1)S(1)} %collective-permute-done.7.refs_3_), channel_id=1, source_target_pairs={{0,24},{8,0},{16,8},{24,16},{1,25},{9,1},{17,9},{25,17},{2,26},{10... | collective-permute-start | bytes 1572872 | tf_op jit(solution)/shard_map/ppermute | solution.py:16
  94.0 18.1 %collective-permute-start.16 = (bf16[2,32,16,256]{3,2,1,0:T(8,128)(2,1)S(1)}, bf16[2,32,16,256]{3,2,1,0:T(8,128)(2,1)}, u32[]{:S(2)}, u32[]{:S(2)}) collective-permute-start(bf16[2,32,16,256]{3,2,1,0:T(8,128)(2,1)S(1)} %collective-permute-done.8.refs_4_), channel_id=1, source_target_pairs={{0,24},{8,0},{16,8},{24,16},{1,25},{9,1},{17,9},{25,17},{2,26},{10... | collective-permute-start | bytes 1572872 | tf_op jit(solution)/shard_map/ppermute | solution.py:16
  95.8 21.9 %collective-permute-start.17 = (bf16[2,32,16,256]{3,2,1,0:T(8,128)(2,1)S(1)}, bf16[2,32,16,256]{3,2,1,0:T(8,128)(2,1)}, u32[]{:S(2)}, u32[]{:S(2)}) collective-permute-start(bf16[2,32,16,256]{3,2,1,0:T(8,128)(2,1)S(1)} %collective-permute-done.9.refs_5_), channel_id=1, source_target_pairs={{0,24},{8,0},{16,8},{24,16},{1,25},{9,1},{17,9},{25,17},{2,26},{10... | collective-permute-start | bytes 1572872 | tf_op jit(solution)/shard_map/ppermute | solution.py:16
  95.9 27.5 %collective-permute-start.18 = (bf16[2,32,16,256]{3,2,1,0:T(8,128)(2,1)}, bf16[2,32,16,256]{3,2,1,0:T(8,128)(2,1)}, u32[]{:S(2)}, u32[]{:S(2)}) collective-permute-start(bf16[2,32,16,256]{3,2,1,0:T(8,128)(2,1)} %collective-permute-done.10.refs_6_), channel_id=1, source_target_pairs={{0,24},{8,0},{16,8},{24,16},{1,25},{9,1},{17,9},{25,17},{2,26},{10... | collective-permute-start | bytes 1572872 | tf_op jit(solution)/shard_map/ppermute | solution.py:16
  100.9 30.0 %collective-permute-start.19 = (bf16[2,32,16,256]{3,2,1,0:T(8,128)(2,1)}, bf16[2,32,16,256]{3,2,1,0:T(8,128)(2,1)}, u32[]{:S(2)}, u32[]{:S(2)}) collective-permute-start(bf16[2,32,16,256]{3,2,1,0:T(8,128)(2,1)} %collective-permute-done.11.refs_7_), channel_id=1, source_target_pairs={{0,24},{8,0},{16,8},{24,16},{1,25},{9,1},{17,9},{25,17},{2,26},{10... | collective-permute-start | bytes 1572872 | tf_op jit(solution)/shard_map/ppermute | solution.py:16
  132.4 7.1 %collective-permute-start.20 = (f32[4,2,32,256]{3,2,1,0:T(8,128)S(1)}, f32[4,2,32,256]{3,2,1,0:T(8,128)S(1)}, u32[]{:S(2)}, u32[]{:S(2)}) collective-permute-start(f32[4,2,32,256]{3,2,1,0:T(8,128)S(1)} %get-tuple-element.28), channel_id=1, source_target_pairs={{0,1},{1,0},{2,3},{3,2},{4,5},{5,4},{6,7},{7,6},{8,9},{9,8},{10,11... | collective-permute-start | bytes 786440 | tf_op jit(solution)/shard_map/ppermute | solution.py:11
  139.6 15.2 %collective-permute-start.21 = (f32[2,2,32,256]{3,2,1,0:T(8,128)S(1)}, f32[2,2,32,256]{3,2,1,0:T(8,128)S(1)}, u32[]{:S(2)}, u32[]{:S(2)}) collective-permute-start(f32[2,2,32,256]{3,2,1,0:T(8,128)S(1)} %slice.35), channel_id=1, source_target_pairs={{0,2},{1,3},{2,0},{3,1},{4,6},{5,7},{6,4},{7,5},{8,10},{9,11},{10,... | collective-permute-start | bytes 393224 | tf_op jit(solution)/shard_map/ppermute | solution.py:11
  154.8 7.2 %collective-permute-start.22 = (f32[1,2,32,256]{3,2,1,0:T(8,128)S(1)}, f32[1,2,32,256]{3,2,1,0:T(8,128)S(1)}, u32[]{:S(2)}, u32[]{:S(2)}) collective-permute-start(f32[1,2,32,256]{3,2,1,0:T(8,128)S(1)} %slice.42), channel_id=1, source_target_pairs={{0,4},{1,5},{2,6},{3,7},{4,0},{5,1},{6,2},{7,3},{8,12},{9,13},{10,... | collective-permute-start | bytes 196616 | tf_op jit(solution)/shard_map/ppermute | solution.py:11

commit v2 on v1

--- a/solution.py
+++ b/solution.py
@@ -24,28 +24,18 @@
         return [lax.dynamic_index_in_dim(cut, me ^ d, 0, False) for d in range(groups)]
     step = 4 if slots % 4 == 0 else 1
 
-    def body(select_ref, x_ref, *refs):
-        outs, held, sem = refs[:groups], refs[groups], refs[groups + 1]
-        copies = [
-            pltpu.make_async_copy(
-                x_ref.at[pl.ds(i * step, step)], held.at[pl.ds(i * step, step)], sem.at[i]
-            )
-            for i in range(slots // step)
-        ]
-        for copy in copies:
-            copy.start()
-        for i, copy in enumerate(copies):
-            copy.wait()
-            for s in range(i * step, (i + 1) * step):
-                for c in range(2):
-                    turned = lax.dot_general(
-                        select_ref[...],
-                        held[s, c],
-                        (((1,), (1,)), ((), ())),
-                        preferred_element_type=jnp.float32,
-                    ).astype(jnp.bfloat16)
-                    for d in range(groups):
-                        outs[d][c, s] = turned[d * part : (d + 1) * part]
+    def body(select_ref, x_ref, *outs):
+        place = pl.program_id(0) * step
+        for s in range(step):
+            for c in range(2):
+                turned = lax.dot_general(
+                    select_ref[...],
+                    x_ref[s, c],
+                    (((1,), (1,)), ((), ())),
+                    preferred_element_type=jnp.float32,
+                ).astype(jnp.bfloat16)
+                for d in range(groups):
+                    outs[d][c, place + s] = turned[d * part : (d + 1) * part]
 
     row = jnp.arange(waves, dtype=jnp.int32)
     source = ((row // part) ^ me) * part + row % part
@@ -53,14 +43,11 @@
     near = pl.BlockSpec(memory_space=pltpu.VMEM)
     return pl.pallas_call(
         body,
-        in_specs=[near, pl.BlockSpec(memory_space=pltpu.HBM)],
+        grid=(slots // step,),
+        in_specs=[near, pl.BlockSpec((step, 2, bands, waves), lambda i: (i, 0, 0, 0))],
         out_specs=[near] * groups,
         out_shape=[jax.ShapeDtypeStruct((2, slots, part, bands), jnp.bfloat16)] * groups,
-        scratch_shapes=[
-            pltpu.VMEM((slots, 2, bands, waves), jnp.bfloat16),
-            pltpu.SemaphoreType.DMA((slots // step,)),
-        ],
-        compiler_params=pltpu.CompilerParams(vmem_limit_bytes=24 << 20),
+        compiler_params=pltpu.CompilerParams(vmem_limit_bytes=48 << 20),
         cost_estimate=pl.CostEstimate(
             flops=4 * slots * waves * waves * bands, bytes_accessed=x.size * 4, transcendentals=0
         ),
@@ -69,12 +56,12 @@
 
 def passed_around(mine, groups):
     rows = [mine]
-    for d in range(2, groups, 2):
+    for d in range(1, groups):
         rows.append(swapped_with(mine, d))
     return rows
 
 
-def pair_lists(bra_info, ket_info, groups, slots, me):
+def pair_list(bra_info, ket_info, groups, slots, me):
     counts = bra_info[:, 0]
     maps = ket_info[:, 1:].reshape(groups, 3, slots)
     device, slot, anchor = (maps[:, i].reshape(groups * slots) for i in range(3))
@@ -84,9 +71,7 @@
     live = (number % slots).reshape(groups, slots) < counts[:, None]
     agreeing = (anchor[:, None] == here[None, :]) & (lands[None, :] == here[:, None])
     agreeing &= live.reshape(-1)[:, None]
-    ket_of = jnp.max(jnp.where(agreeing, number[None, :], -1), axis=1)
-    bra_of = jnp.max(jnp.where(agreeing, number[:, None], -1), axis=0)
-    return ket_of, bra_of
+    return jnp.max(jnp.where(agreeing, number[None, :], -1), axis=1)
 
 
 def multiply_plainly(bras, kets, ket_of, me, groups, scale):
@@ -104,7 +89,7 @@
     return total[1::2], total[0::2]
 
 
-def multiply(bras, kets, ket_of, bra_of, me, groups, scale):
+def multiply(bras, kets, ket_of, me, groups, scale):
     _, slots, part, bands = bras[0].shape
     rows = bands // groups
     depth = slots * part
@@ -122,9 +107,10 @@
     def flat(ket_ref):
         return ket_ref[...].reshape(2 * depth, bands)
 
-    def most(ket_of_ref, bra_of_ref, *refs):
+    def most(ket_of_ref, *refs):
         bra_refs, ket_refs = refs[:groups], refs[groups : groups + early]
         total_ref, last_ref, chosen = refs[groups + early :]
+        chosen[...] = jnp.zeros_like(chosen)
         for d in range(groups):
 
             def put(s, _, d=d):
@@ -135,16 +121,6 @@
                 return 0
 
             lax.fori_loop(0, slots, put, 0, unroll=8)
-
-        def clear(row, _):
-            @pl.when(bra_of_ref[row] < 0)
-            def _():
-                for c in range(2):
-                    chosen[c, row] = jnp.zeros((part, bands), jnp.bfloat16)
-
-            return 0
-
-        lax.fori_loop(0, groups * slots, clear, 0, unroll=8)
         for d in range(early):
             product = jnp.dot(turned(chosen, d), flat(ket_refs[d]), preferred_element_type=jnp.float32)
             if d == 0:
@@ -166,7 +142,7 @@
     flops = 8 * depth * bands * bands
     total, last = pl.pallas_call(
         most,
-        in_specs=[scalar, scalar] + [near] * (groups + early),
+        in_specs=[scalar] + [near] * (groups + early),
         out_specs=[near, near],
         out_shape=[
             jax.ShapeDtypeStruct((2 * bands, bands), jnp.float32),
@@ -175,7 +151,7 @@
         scratch_shapes=[pltpu.VMEM((2, groups * slots + 1, part, bands), jnp.bfloat16)],
         compiler_params=pltpu.CompilerParams(vmem_limit_bytes=32 << 20),
         cost_estimate=pl.CostEstimate(flops=early * flops, bytes_accessed=1 << 20, transcendentals=0),
-    )(ket_of, bra_of, *bras, *kets[:early])
+    )(ket_of, *bras, *kets[:early])
     half = jax.ShapeDtypeStruct((groups // 2, 2, rows, bands), jnp.float32)
     return pl.pallas_call(
         rest,
@@ -223,16 +199,14 @@
         anchor = zero_like(anchor)
         if place == len(arrivals) - 2:
             before_last = anchor
-        if place == groups // 2:
-            even = jnp.stack(info) + anchor
-    odd = swapped_with(even, 1)
-    bra_info = jnp.stack([even, odd], axis=1).reshape(groups, mine.shape[0])
+        if place == 2:
+            bra_info = jnp.stack(info) + anchor
     ket_info = to_previous_pool(bra_info)
-    ket_of, bra_of = pair_lists(bra_info, ket_info + before_last, groups, slots, me)
+    ket_of = pair_list(bra_info, ket_info + before_last, groups, slots, me)
     if (waves // groups) % 16:
         give, keep = multiply_plainly(bras, kets, ket_of, me, groups, scale)
     else:
-        give, keep = multiply(bras, kets, ket_of, bra_of, me, groups, scale)
+        give, keep = multiply(bras, kets, ket_of, me, groups, scale)
     distance = 1
     while True:
         keep = keep + swapped_with(give, distance)

time: 163 us -> 169 us (1.037)
  starting transfers between devices: 39.5 us -> 70.7 us
  waiting for transfers between devices: 96.8 us -> 69.8 us
    ppermute x9, starting transfers between devices: 8.44 us -> 39.2 us  [to_previous_pool(): lax.ppermute(value, 'pool', [(i, (i - 1) % count) for i in range(count)])]
    ppermute x14 -> x17, waiting for transfers between devices: 67.9 us -> 43.2 us  [swapped_with(): return lax.ppermute(value, 'ga', [(i, i ^ distance) for i in range(count)])]
    ppermute x9, waiting for transfers between devices: 28.9 us -> 26.6 us  [to_previous_pool(): lax.ppermute(value, 'pool', [(i, (i - 1) % count) for i in range(count)])]
    ppermute x14 -> x17, starting transfers between devices: 31.1 us -> 31.5 us  [swapped_with(): return lax.ppermute(value, 'ga', [(i, i ^ distance) for i in range(count)])]
  transfers between devices with their start and end apart: 23 -> 26, of which waited for: 13 -> 13; matrix products, arithmetic and copies ran while one was open for 2% -> 1% of each run, Pallas kernels for 11% -> 11%
where the time goes in v2:
time: 169 us; the launch traced here: 168 us
  starting transfers between devices  70.7 us (42%)
  waiting for transfers between devices  69.8 us (41%)
  Pallas kernels  20.4 us (12%)
  other arithmetic  3.15 us (2%)
  local copies, waits for them, and re-layouts  2.99 us (2%)
    ppermute x17, waiting for transfers between devices, swapped_with(): return lax.ppermute(value, 'ga', [(i, i ^ distance) for i in range(count)])  43.2 us
    ppermute x9, starting transfers between devices, to_previous_pool(): lax.ppermute(value, 'pool', [(i, (i - 1) % count) for i in range(count)])  39.2 us
    ppermute x17, starting transfers between devices, swapped_with(): return lax.ppermute(value, 'ga', [(i, i ^ distance) for i in range(count)])  31.5 us
    ppermute x9, waiting for transfers between devices, to_previous_pool(): lax.ppermute(value, 'pool', [(i, (i - 1) % count) for i in range(count)])  26.6 us
    pallas_call x1, Pallas kernels, pack(): pl.pallas_call(body, grid=(slots // step,), in_specs=[near, pl.BlockSpec(...  7.11 us
    pallas_call x6, Pallas kernels, zero_like(): pl.pallas_call(body, in_specs=[scalar], out_specs=scalar, out_shape=jax.S...  6.38 us
    pallas_call x1, Pallas kernels, multiply(): pl.pallas_call(most, in_specs=[scalar] + [near] * (groups + early), out_s...  5.38 us
  transfers between devices with their start and end apart: 26, of which 13 were waited for; matrix products, arithmetic and copies ran while one was open for 1% of the time, Pallas kernels for 11%

profile of v2, /device:TPU:1, one launch (start us, length us, event | category | flops | bytes accessed | tf_op | source)
XLA Modules:
  0.0 167.9 jit_solution(9503048210769114086)
XLA Ops:
  1.4 2.0 %collective-permute-start = (s32[97]{0:T(128)S(1)}, s32[97]{0:T(128)S(1)}, u32[]{:S(2)}, u32[]{:S(2)}) collective-permute-start(s32[97]{0:T(128)S(1)} %bitcast.14), channel_id=1, source_target_pairs={{0,1},{1,0},{2,3},{3,2},{4,5},{5,4},{6,7},{7,6},{8,9},{9,8},{10,11... | collective-permute-start | bytes 1172 | tf_op jit(solution)/shard_map/ppermute | solution.py:11
  3.4 1.3 collective-permute-start.1
  4.7 2.4 %collective-permute-start.3 = (s32[97]{0:T(128)S(1)}, s32[97]{0:T(128)S(1)}, u32[]{:S(2)}, u32[]{:S(2)}) collective-permute-start(s32[97]{0:T(128)S(1)} %bitcast.17), channel_id=1, source_target_pairs={{0,4},{1,5},{2,6},{3,7},{4,0},{5,1},{6,2},{7,3},{8,12},{9,13},{10,... | collective-permute-start | bytes 1172 | tf_op jit(solution)/shard_map/ppermute | solution.py:11
  8.3 7.1 %shard_map.61 = (bf16[2,32,16,256]{3,2,1,0:T(8,128)(2,1)S(1)}, bf16[2,32,16,256]{3,2,1,0:T(8,128)(2,1)}, bf16[2,32,16,256]{3,2,1,0:T(8,128)(2,1)}, bf16[2,32,16,...) custom-call(bf16[128,128]{1,0:T(8,128)(2,1)S(1)} %fusion.select_ref,, ...), custom_call_target="tpu_custom_call" | custom-call | flops 536870912 | bytes 8388608 | tf_op jit(solution)/shard_map/pallas_call | solution.py:44
  18.3 1.2 shard_map.56._
  19.5 1.1 shard_map.57._
  20.6 3.4 %collective-permute-start.5 = (s32[97]{0:T(128)S(1)}, s32[97]{0:T(128)S(1)}, u32[]{:S(2)}, u32[]{:S(2)}) collective-permute-start(s32[97]{0:T(128)S(1)} %bitcast.19), channel_id=1, source_target_pairs={{0,6},{1,7},{2,4},{3,5},{4,2},{5,3},{6,0},{7,1},{8,14},{9,15},{10,... | collective-permute-start | bytes 1172 | tf_op jit(solution)/shard_map/ppermute | solution.py:11
  24.1 1.2 collective-permute-start.8
  25.3 1.4 collective-permute-start.10
  26.8 2.1 %collective-permute-start.11 = (bf16[2,32,16,256]{3,2,1,0:T(8,128)(2,1)}, bf16[2,32,16,256]{3,2,1,0:T(8,128)(2,1)S(1)}, u32[]{:S(2)}, u32[]{:S(2)}) collective-permute-start(bf16[2,32,16,256]{3,2,1,0:T(8,128)(2,1)} %get-tuple-element.21), channel_id=1, source_target_pairs={{0,4},{1,5},{2,6},{3,7},{4,0},{5,1},{6,2},{7,3},{8,12},{9,13},{10,... | collective-permute-start | bytes 1572872 | tf_op jit(solution)/shard_map/ppermute | solution.py:11
  29.9 3.7 %collective-permute-start.7 = (s32[8,97]{1,0:T(8,128)S(1)}, s32[8,97]{1,0:T(8,128)S(1)}, u32[]{:S(2)}, u32[]{:S(2)}) collective-permute-start(s32[8,97]{1,0:T(8,128)S(1)} %broadcast_add_fusion.1), channel_id=1, source_target_pairs={{0,24},{8,0},{16,8},{24,16},{1,25},{9,1},{17,9},{25,17},{2,26},{10... | collective-permute-start | bytes 9320 | tf_op jit(solution)/shard_map/ppermute | solution.py:16
  33.5 2.7 %collective-permute-done.7 = s32[8,97]{1,0:T(8,128)S(1)} collective-permute-done((s32[8,97]{1,0:T(8,128)S(1)}, s32[8,97]{1,0:T(8,128)S(1)}, u32[]{:S(2)}, u32[]{:S(2)}) %collective-permute-start.7) | collective-permute-done | bytes 3136 | tf_op jit(solution)/shard_map/ppermute | solution.py:16
  37.1 3.3 %collective-permute-start.13 = (bf16[2,32,16,256]{3,2,1,0:T(8,128)(2,1)}, bf16[2,32,16,256]{3,2,1,0:T(8,128)(2,1)}, u32[]{:S(2)}, u32[]{:S(2)}) collective-permute-start(bf16[2,32,16,256]{3,2,1,0:T(8,128)(2,1)} %copy-done.1), channel_id=1, source_target_pairs={{0,6},{1,7},{2,4},{3,5},{4,2},{5,3},{6,0},{7,1},{8,14},{9,15},{10,... | collective-permute-start | bytes 1572872 | tf_op jit(solution)/shard_map/ppermute | solution.py:11
  40.5 18.1 %collective-permute-done.9.refs_2_ = bf16[2,32,16,256]{3,2,1,0:T(8,128)(2,1)S(1)} collective-permute-done((bf16[2,32,16,256]{3,2,1,0:T(8,128)(2,1)}, bf16[2,32,16,256]{3,2,1,0:T(8,128)(2,1)S(1)}, u32[]{:S(2)}, u32[]{:S(2)}) %collective-permute-start.9) | collective-permute-done | bytes 524320 | tf_op jit(solution)/shard_map/ppermute | solution.py:11
  58.5 9.9 %collective-permute-done.10.refs_3_ = bf16[2,32,16,256]{3,2,1,0:T(8,128)(2,1)S(1)} collective-permute-done((bf16[2,32,16,256]{3,2,1,0:T(8,128)(2,1)}, bf16[2,32,16,256]{3,2,1,0:T(8,128)(2,1)S(1)}, u32[]{:S(2)}, u32[]{:S(2)}) %collective-permute-start.10) | collective-permute-done | bytes 524320 | tf_op jit(solution)/shard_map/ppermute | solution.py:11
  68.4 3.5 %collective-permute-start.15 = (bf16[2,32,16,256]{3,2,1,0:T(8,128)(2,1)S(1)}, bf16[2,32,16,256]{3,2,1,0:T(8,128)(2,1)}, u32[]{:S(2)}, u32[]{:S(2)}) collective-permute-start(bf16[2,32,16,256]{3,2,1,0:T(8,128)(2,1)S(1)} %get-tuple-element.17.refs_0_), channel_id=1, source_target_pairs={{0,24},{8,0},{16,8},{24,16},{1,25},{9,1},{17,9},{25,17},{2,26},{10... | collective-permute-start | bytes 1572872 | tf_op jit(solution)/shard_map/ppermute | solution.py:16
  71.9 29.3 %collective-permute-start.17 = (bf16[2,32,16,256]{3,2,1,0:T(8,128)(2,1)S(1)}, bf16[2,32,16,256]{3,2,1,0:T(8,128)(2,1)}, u32[]{:S(2)}, u32[]{:S(2)}) collective-permute-start(bf16[2,32,16,256]{3,2,1,0:T(8,128)(2,1)S(1)} %collective-permute-done.9.refs_2_), channel_id=1, source_target_pairs={{0,24},{8,0},{16,8},{24,16},{1,25},{9,1},{17,9},{25,17},{2,26},{10... | collective-permute-start | bytes 1572872 | tf_op jit(solution)/shard_map/ppermute | solution.py:16
  101.2 1.2 shard_map.58._
  103.5 1.2 shard_map.60
  105.0 2.7 %collective-permute-start.19 = (bf16[2,32,16,256]{3,2,1,0:T(8,128)(2,1)S(1)}, bf16[2,32,16,256]{3,2,1,0:T(8,128)(2,1)}, u32[]{:S(2)}, u32[]{:S(2)}) collective-permute-start(bf16[2,32,16,256]{3,2,1,0:T(8,128)(2,1)S(1)} %collective-permute-done.11.refs_4_), channel_id=1, source_target_pairs={{0,24},{8,0},{16,8},{24,16},{1,25},{9,1},{17,9},{25,17},{2,26},{10... | collective-permute-start | bytes 1572872 | tf_op jit(solution)/shard_map/ppermute | solution.py:16
  107.8 2.5 %collective-permute-done.17.refs_10_ = bf16[2,32,16,256]{3,2,1,0:T(8,128)(2,1)} collective-permute-done((bf16[2,32,16,256]{3,2,1,0:T(8,128)(2,1)S(1)}, bf16[2,32,16,256]{3,2,1,0:T(8,128)(2,1)}, u32[]{:S(2)}, u32[]{:S(2)}) %collective-permute-start.17) | collective-permute-done | bytes 524320 | tf_op jit(solution)/shard_map/ppermute | solution.py:16
  111.5 4.4 %collective-permute-done.18.refs_11_ = bf16[2,32,16,256]{3,2,1,0:T(8,128)(2,1)} collective-permute-done((bf16[2,32,16,256]{3,2,1,0:T(8,128)(2,1)S(1)}, bf16[2,32,16,256]{3,2,1,0:T(8,128)(2,1)}, u32[]{:S(2)}, u32[]{:S(2)}) %collective-permute-start.18) | collective-permute-done | bytes 524320 | tf_op jit(solution)/shard_map/ppermute | solution.py:16
  115.9 5.6 %collective-permute-done.19.refs_12_ = bf16[2,32,16,256]{3,2,1,0:T(8,128)(2,1)} collective-permute-done((bf16[2,32,16,256]{3,2,1,0:T(8,128)(2,1)S(1)}, bf16[2,32,16,256]{3,2,1,0:T(8,128)(2,1)}, u32[]{:S(2)}, u32[]{:S(2)}) %collective-permute-start.19) | collective-permute-done | bytes 524320 | tf_op jit(solution)/shard_map/ppermute | solution.py:16
  121.5 5.6 %collective-permute-done.20.refs_13_ = bf16[2,32,16,256]{3,2,1,0:T(8,128)(2,1)} collective-permute-done((bf16[2,32,16,256]{3,2,1,0:T(8,128)(2,1)S(1)}, bf16[2,32,16,256]{3,2,1,0:T(8,128)(2,1)}, u32[]{:S(2)}, u32[]{:S(2)}) %collective-permute-start.20) | collective-permute-done | bytes 524320 | tf_op jit(solution)/shard_map/ppermute | solution.py:16
  127.1 5.6 %collective-permute-done.21.refs_14_ = bf16[2,32,16,256]{3,2,1,0:T(8,128)(2,1)} collective-permute-done((bf16[2,32,16,256]{3,2,1,0:T(8,128)(2,1)}, bf16[2,32,16,256]{3,2,1,0:T(8,128)(2,1)}, u32[]{:S(2)}, u32[]{:S(2)}) %collective-permute-start.21) | collective-permute-done | bytes 524320 | tf_op jit(solution)/shard_map/ppermute | solution.py:16
  132.8 5.4 %shard_map.62 = (f32[512,256]{1,0:T(8,128)S(1)}, bf16[512,1024]{1,0:T(8,128)(2,1)S(1)}) custom-call(s32[256]{0:T(256)S(1)} %select_reduce_fusion.ket_of_ref, bf16[2,32,16,256]{3,2,1,0:T(8,128)(2,1)S(1)} %get-tuple-element.17.refs_0_, bf16[2,32,16,256]{3,2,1,0:T(8,128)(2,1)S(1)} %collective-permute-done.8.refs_1_, ...), custom_call_target="tpu_custom_call" | custom-call | flops 1879048192 | bytes 1048576 | tf_op jit(solution)/shard_map/pallas_call | solution.py:143
  138.4 1.5 shard_map.63
  140.0 7.0 %collective-permute-done.23 = f32[4,2,32,256]{3,2,1,0:T(8,128)S(1)} collective-permute-done((f32[4,2,32,256]{3,2,1,0:T(8,128)S(1)}, f32[4,2,32,256]{3,2,1,0:T(8,128)S(1)}, u32[]{:S(2)}, u32[]{:S(2)}) %collective-permute-start.23) | collective-permute-done | bytes 262176 | tf_op jit(solution)/shard_map/ppermute | solution.py:11
  147.1 9.0 %collective-permute-start.24 = (f32[2,2,32,256]{3,2,1,0:T(8,128)S(1)}, f32[2,2,32,256]{3,2,1,0:T(8,128)S(1)}, u32[]{:S(2)}, u32[]{:S(2)}) collective-permute-start(f32[2,2,32,256]{3,2,1,0:T(8,128)S(1)} %slice.35), channel_id=1, source_target_pairs={{0,2},{1,3},{2,0},{3,1},{4,6},{5,7},{6,4},{7,5},{8,10},{9,11},{10,... | collective-permute-start | bytes 393224 | tf_op jit(solution)/shard_map/ppermute | solution.py:11
  156.1 4.0 %collective-permute-done.24 = f32[2,2,32,256]{3,2,1,0:T(8,128)S(1)} collective-permute-done((f32[2,2,32,256]{3,2,1,0:T(8,128)S(1)}, f32[2,2,32,256]{3,2,1,0:T(8,128)S(1)}, u32[]{:S(2)}, u32[]{:S(2)}) %collective-permute-start.24) | collective-permute-done | bytes 131104 | tf_op jit(solution)/shard_map/ppermute | solution.py:11
  160.1 3.2 %collective-permute-start.25 = (f32[1,2,32,256]{3,2,1,0:T(8,128)S(1)}, f32[1,2,32,256]{3,2,1,0:T(8,128)S(1)}, u32[]{:S(2)}, u32[]{:S(2)}) collective-permute-start(f32[1,2,32,256]{3,2,1,0:T(8,128)S(1)} %slice.42), channel_id=1, source_target_pairs={{0,4},{1,5},{2,6},{3,7},{4,0},{5,1},{6,2},{7,3},{8,12},{9,13},{10,... | collective-permute-start | bytes 196616 | tf_op jit(solution)/shard_map/ppermute | solution.py:11
  163.4 3.9 %collective-permute-done.25 = f32[1,2,32,256]{3,2,1,0:T(8,128)S(1)} collective-permute-done((f32[1,2,32,256]{3,2,1,0:T(8,128)S(1)}, f32[1,2,32,256]{3,2,1,0:T(8,128)S(1)}, u32[]{:S(2)}, u32[]{:S(2)}) %collective-permute-start.25) | collective-permute-done | bytes 65568 | tf_op jit(solution)/shard_map/ppermute | solution.py:11
  (57 shorter events, 10.5 us)
Async XLA Ops:
  1.4 19.2 %collective-permute-start = (s32[97]{0:T(128)S(1)}, s32[97]{0:T(128)S(1)}, u32[]{:S(2)}, u32[]{:S(2)}) collective-permute-start(s32[97]{0:T(128)S(1)} %bitcast.14), channel_id=1, source_target_pairs={{0,1},{1,0},{2,3},{3,2},{4,5},{5,4},{6,7},{7,6},{8,9},{9,8},{10,11... | collective-permute-start | bytes 1172 | tf_op jit(solution)/shard_map/ppermute | solution.py:11
  3.4 20.6 %collective-permute-start.1 = (s32[97]{0:T(128)S(1)}, s32[97]{0:T(128)S(1)}, u32[]{:S(2)}, u32[]{:S(2)}) collective-permute-start(s32[97]{0:T(128)S(1)} %bitcast.15), channel_id=1, source_target_pairs={{0,2},{1,3},{2,0},{3,1},{4,6},{5,7},{6,4},{7,5},{8,10},{9,11},{10,... | collective-permute-start | bytes 1172 | tf_op jit(solution)/shard_map/ppermute | solution.py:11
  4.7 19.4 %collective-permute-start.2 = (s32[97]{0:T(128)S(1)}, s32[97]{0:T(128)S(1)}, u32[]{:S(2)}, u32[]{:S(2)}) collective-permute-start(s32[97]{0:T(128)S(1)} %bitcast.16), channel_id=1, source_target_pairs={{0,3},{1,2},{2,1},{3,0},{4,7},{5,6},{6,5},{7,4},{8,11},{9,10},{10,... | collective-permute-start | bytes 1172 | tf_op jit(solution)/shard_map/ppermute | solution.py:11
  4.7 20.6 %collective-permute-start.3 = (s32[97]{0:T(128)S(1)}, s32[97]{0:T(128)S(1)}, u32[]{:S(2)}, u32[]{:S(2)}) collective-permute-start(s32[97]{0:T(128)S(1)} %bitcast.17), channel_id=1, source_target_pairs={{0,4},{1,5},{2,6},{3,7},{4,0},{5,1},{6,2},{7,3},{8,12},{9,13},{10,... | collective-permute-start | bytes 1172 | tf_op jit(solution)/shard_map/ppermute | solution.py:11
  7.2 18.1 %collective-permute-start.4 = (s32[97]{0:T(128)S(1)}, s32[97]{0:T(128)S(1)}, u32[]{:S(2)}, u32[]{:S(2)}) collective-permute-start(s32[97]{0:T(128)S(1)} %bitcast.18), channel_id=1, source_target_pairs={{0,5},{1,4},{2,7},{3,6},{4,1},{5,0},{6,3},{7,2},{8,13},{9,12},{10,... | collective-permute-start | bytes 1172 | tf_op jit(solution)/shard_map/ppermute | solution.py:11
  15.4 0.8 copy-start
  16.2 0.8 copy-start.1
  17.0 0.8 copy-start.2
  20.6 6.1 %collective-permute-start.5 = (s32[97]{0:T(128)S(1)}, s32[97]{0:T(128)S(1)}, u32[]{:S(2)}, u32[]{:S(2)}) collective-permute-start(s32[97]{0:T(128)S(1)} %bitcast.19), channel_id=1, source_target_pairs={{0,6},{1,7},{2,4},{3,5},{4,2},{5,3},{6,0},{7,1},{8,14},{9,15},{10,... | collective-permute-start | bytes 1172 | tf_op jit(solution)/shard_map/ppermute | solution.py:11
  24.0 5.1 %collective-permute-start.6 = (s32[97]{0:T(128)S(1)}, s32[97]{0:T(128)S(1)}, u32[]{:S(2)}, u32[]{:S(2)}) collective-permute-start(s32[97]{0:T(128)S(1)} %bitcast.20), channel_id=1, source_target_pairs={{0,7},{1,6},{2,5},{3,4},{4,3},{5,2},{6,1},{7,0},{8,15},{9,14},{10,... | collective-permute-start | bytes 1172 | tf_op jit(solution)/shard_map/ppermute | solution.py:11
  24.1 13.1 %collective-permute-start.8 = (bf16[2,32,16,256]{3,2,1,0:T(8,128)(2,1)}, bf16[2,32,16,256]{3,2,1,0:T(8,128)(2,1)S(1)}, u32[]{:S(2)}, u32[]{:S(2)}) collective-permute-start(bf16[2,32,16,256]{3,2,1,0:T(8,128)(2,1)} %get-tuple-element.18), channel_id=1, source_target_pairs={{0,1},{1,0},{2,3},{3,2},{4,5},{5,4},{6,7},{7,6},{8,9},{9,8},{10,11... | collective-permute-start | bytes 1572872 | tf_op jit(solution)/shard_map/ppermute | solution.py:11
  25.3 33.2 %collective-permute-start.9 = (bf16[2,32,16,256]{3,2,1,0:T(8,128)(2,1)}, bf16[2,32,16,256]{3,2,1,0:T(8,128)(2,1)S(1)}, u32[]{:S(2)}, u32[]{:S(2)}) collective-permute-start(bf16[2,32,16,256]{3,2,1,0:T(8,128)(2,1)} %get-tuple-element.19), channel_id=1, source_target_pairs={{0,2},{1,3},{2,0},{3,1},{4,6},{5,7},{6,4},{7,5},{8,10},{9,11},{10,... | collective-permute-start | bytes 1572872 | tf_op jit(solution)/shard_map/ppermute | solution.py:11
  25.3 43.1 %collective-permute-start.10 = (bf16[2,32,16,256]{3,2,1,0:T(8,128)(2,1)}, bf16[2,32,16,256]{3,2,1,0:T(8,128)(2,1)S(1)}, u32[]{:S(2)}, u32[]{:S(2)}) collective-permute-start(bf16[2,32,16,256]{3,2,1,0:T(8,128)(2,1)} %get-tuple-element.20), channel_id=1, source_target_pairs={{0,3},{1,2},{2,1},{3,0},{4,7},{5,6},{6,5},{7,4},{8,11},{9,10},{10,... | collective-permute-start | bytes 1572872 | tf_op jit(solution)/shard_map/ppermute | solution.py:11
  26.8 45.1 %collective-permute-start.11 = (bf16[2,32,16,256]{3,2,1,0:T(8,128)(2,1)}, bf16[2,32,16,256]{3,2,1,0:T(8,128)(2,1)S(1)}, u32[]{:S(2)}, u32[]{:S(2)}) collective-permute-start(bf16[2,32,16,256]{3,2,1,0:T(8,128)(2,1)} %get-tuple-element.21), channel_id=1, source_target_pairs={{0,4},{1,5},{2,6},{3,7},{4,0},{5,1},{6,2},{7,3},{8,12},{9,13},{10,... | collective-permute-start | bytes 1572872 | tf_op jit(solution)/shard_map/ppermute | solution.py:11
  29.9 6.4 %collective-permute-start.7 = (s32[8,97]{1,0:T(8,128)S(1)}, s32[8,97]{1,0:T(8,128)S(1)}, u32[]{:S(2)}, u32[]{:S(2)}) collective-permute-start(s32[8,97]{1,0:T(8,128)S(1)} %broadcast_add_fusion.1), channel_id=1, source_target_pairs={{0,24},{8,0},{16,8},{24,16},{1,25},{9,1},{17,9},{25,17},{2,26},{10... | collective-permute-start | bytes 9320 | tf_op jit(solution)/shard_map/ppermute | solution.py:16
  36.3 35.6 %collective-permute-start.12 = (bf16[2,32,16,256]{3,2,1,0:T(8,128)(2,1)}, bf16[2,32,16,256]{3,2,1,0:T(8,128)(2,1)S(1)}, u32[]{:S(2)}, u32[]{:S(2)}) collective-permute-start(bf16[2,32,16,256]{3,2,1,0:T(8,128)(2,1)} %copy-done.2), channel_id=1, source_target_pairs={{0,5},{1,4},{2,7},{3,6},{4,1},{5,0},{6,3},{7,2},{8,13},{9,12},{10,... | collective-permute-start | bytes 1572872 | tf_op jit(solution)/shard_map/ppermute | solution.py:11
  37.1 67.9 %collective-permute-start.13 = (bf16[2,32,16,256]{3,2,1,0:T(8,128)(2,1)}, bf16[2,32,16,256]{3,2,1,0:T(8,128)(2,1)}, u32[]{:S(2)}, u32[]{:S(2)}) collective-permute-start(bf16[2,32,16,256]{3,2,1,0:T(8,128)(2,1)} %copy-done.1), channel_id=1, source_target_pairs={{0,6},{1,7},{2,4},{3,5},{4,2},{5,3},{6,0},{7,1},{8,14},{9,15},{10,... | collective-permute-start | bytes 1572872 | tf_op jit(solution)/shard_map/ppermute | solution.py:11
  58.5 46.5 %collective-permute-start.14 = (bf16[2,32,16,256]{3,2,1,0:T(8,128)(2,1)}, bf16[2,32,16,256]{3,2,1,0:T(8,128)(2,1)}, u32[]{:S(2)}, u32[]{:S(2)}) collective-permute-start(bf16[2,32,16,256]{3,2,1,0:T(8,128)(2,1)} %copy-done), channel_id=1, source_target_pairs={{0,7},{1,6},{2,5},{3,4},{4,3},{5,2},{6,1},{7,0},{8,15},{9,14},{10,... | collective-permute-start | bytes 1572872 | tf_op jit(solution)/shard_map/ppermute | solution.py:11
  68.4 39.3 %collective-permute-start.15 = (bf16[2,32,16,256]{3,2,1,0:T(8,128)(2,1)S(1)}, bf16[2,32,16,256]{3,2,1,0:T(8,128)(2,1)}, u32[]{:S(2)}, u32[]{:S(2)}) collective-permute-start(bf16[2,32,16,256]{3,2,1,0:T(8,128)(2,1)S(1)} %get-tuple-element.17.refs_0_), channel_id=1, source_target_pairs={{0,24},{8,0},{16,8},{24,16},{1,25},{9,1},{17,9},{25,17},{2,26},{10... | collective-permute-start | bytes 1572872 | tf_op jit(solution)/shard_map/ppermute | solution.py:16
  71.9 35.9 %collective-permute-start.16 = (bf16[2,32,16,256]{3,2,1,0:T(8,128)(2,1)S(1)}, bf16[2,32,16,256]{3,2,1,0:T(8,128)(2,1)}, u32[]{:S(2)}, u32[]{:S(2)}) collective-permute-start(bf16[2,32,16,256]{3,2,1,0:T(8,128)(2,1)S(1)} %collective-permute-done.8.refs_1_), channel_id=1, source_target_pairs={{0,24},{8,0},{16,8},{24,16},{1,25},{9,1},{17,9},{25,17},{2,26},{10... | collective-permute-start | bytes 1572872 | tf_op jit(solution)/shard_map/ppermute | solution.py:16
  71.9 38.4 %collective-permute-start.17 = (bf16[2,32,16,256]{3,2,1,0:T(8,128)(2,1)S(1)}, bf16[2,32,16,256]{3,2,1,0:T(8,128)(2,1)}, u32[]{:S(2)}, u32[]{:S(2)}) collective-permute-start(bf16[2,32,16,256]{3,2,1,0:T(8,128)(2,1)S(1)} %collective-permute-done.9.refs_2_), channel_id=1, source_target_pairs={{0,24},{8,0},{16,8},{24,16},{1,25},{9,1},{17,9},{25,17},{2,26},{10... | collective-permute-start | bytes 1572872 | tf_op jit(solution)/shard_map/ppermute | solution.py:16
  105.0 10.9 %collective-permute-start.18 = (bf16[2,32,16,256]{3,2,1,0:T(8,128)(2,1)S(1)}, bf16[2,32,16,256]{3,2,1,0:T(8,128)(2,1)}, u32[]{:S(2)}, u32[]{:S(2)}) collective-permute-start(bf16[2,32,16,256]{3,2,1,0:T(8,128)(2,1)S(1)} %collective-permute-done.10.refs_3_), channel_id=1, source_target_pairs={{0,24},{8,0},{16,8},{24,16},{1,25},{9,1},{17,9},{25,17},{2,26},{10... | collective-permute-start | bytes 1572872 | tf_op jit(solution)/shard_map/ppermute | solution.py:16
  105.0 16.5 %collective-permute-start.19 = (bf16[2,32,16,256]{3,2,1,0:T(8,128)(2,1)S(1)}, bf16[2,32,16,256]{3,2,1,0:T(8,128)(2,1)}, u32[]{:S(2)}, u32[]{:S(2)}) collective-permute-start(bf16[2,32,16,256]{3,2,1,0:T(8,128)(2,1)S(1)} %collective-permute-done.11.refs_4_), channel_id=1, source_target_pairs={{0,24},{8,0},{16,8},{24,16},{1,25},{9,1},{17,9},{25,17},{2,26},{10... | collective-permute-start | bytes 1572872 | tf_op jit(solution)/shard_map/ppermute | solution.py:16
  107.7 19.5 %collective-permute-start.20 = (bf16[2,32,16,256]{3,2,1,0:T(8,128)(2,1)S(1)}, bf16[2,32,16,256]{3,2,1,0:T(8,128)(2,1)}, u32[]{:S(2)}, u32[]{:S(2)}) collective-permute-start(bf16[2,32,16,256]{3,2,1,0:T(8,128)(2,1)S(1)} %collective-permute-done.12.refs_5_), channel_id=1, source_target_pairs={{0,24},{8,0},{16,8},{24,16},{1,25},{9,1},{17,9},{25,17},{2,26},{10... | collective-permute-start | bytes 1572872 | tf_op jit(solution)/shard_map/ppermute | solution.py:16
  107.8 25.0 %collective-permute-start.21 = (bf16[2,32,16,256]{3,2,1,0:T(8,128)(2,1)}, bf16[2,32,16,256]{3,2,1,0:T(8,128)(2,1)}, u32[]{:S(2)}, u32[]{:S(2)}) collective-permute-start(bf16[2,32,16,256]{3,2,1,0:T(8,128)(2,1)} %collective-permute-done.13.refs_6_), channel_id=1, source_target_pairs={{0,24},{8,0},{16,8},{24,16},{1,25},{9,1},{17,9},{25,17},{2,26},{10... | collective-permute-start | bytes 1572872 | tf_op jit(solution)/shard_map/ppermute | solution.py:16
  110.3 28.1 %collective-permute-start.22 = (bf16[2,32,16,256]{3,2,1,0:T(8,128)(2,1)}, bf16[2,32,16,256]{3,2,1,0:T(8,128)(2,1)}, u32[]{:S(2)}, u32[]{:S(2)}) collective-permute-start(bf16[2,32,16,256]{3,2,1,0:T(8,128)(2,1)} %collective-permute-done.14.refs_7_), channel_id=1, source_target_pairs={{0,24},{8,0},{16,8},{24,16},{1,25},{9,1},{17,9},{25,17},{2,26},{10... | collective-permute-start | bytes 1572872 | tf_op jit(solution)/shard_map/ppermute | solution.py:16
  139.9 7.1 %collective-permute-start.23 = (f32[4,2,32,256]{3,2,1,0:T(8,128)S(1)}, f32[4,2,32,256]{3,2,1,0:T(8,128)S(1)}, u32[]{:S(2)}, u32[]{:S(2)}) collective-permute-start(f32[4,2,32,256]{3,2,1,0:T(8,128)S(1)} %get-tuple-element.28), channel_id=1, source_target_pairs={{0,1},{1,0},{2,3},{3,2},{4,5},{5,4},{6,7},{7,6},{8,9},{9,8},{10,11... | collective-permute-start | bytes 786440 | tf_op jit(solution)/shard_map/ppermute | solution.py:11
  147.1 13.0 %collective-permute-start.24 = (f32[2,2,32,256]{3,2,1,0:T(8,128)S(1)}, f32[2,2,32,256]{3,2,1,0:T(8,128)S(1)}, u32[]{:S(2)}, u32[]{:S(2)}) collective-permute-start(f32[2,2,32,256]{3,2,1,0:T(8,128)S(1)} %slice.35), channel_id=1, source_target_pairs={{0,2},{1,3},{2,0},{3,1},{4,6},{5,7},{6,4},{7,5},{8,10},{9,11},{10,... | collective-permute-start | bytes 393224 | tf_op jit(solution)/shard_map/ppermute | solution.py:11
  160.1 7.1 %collective-permute-start.25 = (f32[1,2,32,256]{3,2,1,0:T(8,128)S(1)}, f32[1,2,32,256]{3,2,1,0:T(8,128)S(1)}, u32[]{:S(2)}, u32[]{:S(2)}) collective-permute-start(f32[1,2,32,256]{3,2,1,0:T(8,128)S(1)} %slice.42), channel_id=1, source_target_pairs={{0,4},{1,5},{2,6},{3,7},{4,0},{5,1},{6,2},{7,3},{8,12},{9,13},{10,... | collective-permute-start | bytes 196616 | tf_op jit(solution)/shard_map/ppermute | solution.py:11

commit v3 on v1

--- a/solution.py
+++ b/solution.py
@@ -60,7 +60,7 @@
             pltpu.VMEM((slots, 2, bands, waves), jnp.bfloat16),
             pltpu.SemaphoreType.DMA((slots // step,)),
         ],
-        compiler_params=pltpu.CompilerParams(vmem_limit_bytes=24 << 20),
+        compiler_params=pltpu.CompilerParams(vmem_limit_bytes=48 << 20),
         cost_estimate=pl.CostEstimate(
             flops=4 * slots * waves * waves * bands, bytes_accessed=x.size * 4, transcendentals=0
         ),
@@ -69,12 +69,12 @@
 
 def passed_around(mine, groups):
     rows = [mine]
-    for d in range(2, groups, 2):
+    for d in range(1, groups):
         rows.append(swapped_with(mine, d))
     return rows
 
 
-def pair_lists(bra_info, ket_info, groups, slots, me):
+def pair_list(bra_info, ket_info, groups, slots, me):
     counts = bra_info[:, 0]
     maps = ket_info[:, 1:].reshape(groups, 3, slots)
     device, slot, anchor = (maps[:, i].reshape(groups * slots) for i in range(3))
@@ -84,9 +84,7 @@
     live = (number % slots).reshape(groups, slots) < counts[:, None]
     agreeing = (anchor[:, None] == here[None, :]) & (lands[None, :] == here[:, None])
     agreeing &= live.reshape(-1)[:, None]
-    ket_of = jnp.max(jnp.where(agreeing, number[None, :], -1), axis=1)
-    bra_of = jnp.max(jnp.where(agreeing, number[:, None], -1), axis=0)
-    return ket_of, bra_of
+    return jnp.max(jnp.where(agreeing, number[None, :], -1), axis=1)
 
 
 def multiply_plainly(bras, kets, ket_of, me, groups, scale):
@@ -99,12 +97,13 @@
         return jnp.einsum("trm,trn->mn", bra[a], ket[b], preferred_element_type=jnp.float32)
 
     total = jnp.stack([dot(0, 0) + dot(1, 1), dot(0, 1) - dot(1, 0)]) * scale
-    total = total.reshape(2, groups, bands // groups, bands).transpose(1, 0, 2, 3)
-    total = total[jnp.arange(groups, dtype=jnp.int32) ^ me]
-    return total[1::2], total[0::2]
-
-
-def multiply(bras, kets, ket_of, bra_of, me, groups, scale):
+    total = total.reshape(2, groups, bands // groups, bands)
+    total = total[:, jnp.arange(groups, dtype=jnp.int32) ^ me]
+    plan = halving_plan(groups)
+    return [total[c][jnp.array(blocks)] for c in range(2) for blocks in plan[c][0]]
+
+
+def multiply(bras, kets, ket_of, me, groups, scale):
     _, slots, part, bands = bras[0].shape
     rows = bands // groups
     depth = slots * part
@@ -122,9 +121,10 @@
     def flat(ket_ref):
         return ket_ref[...].reshape(2 * depth, bands)
 
-    def most(ket_of_ref, bra_of_ref, *refs):
+    def most(ket_of_ref, *refs):
         bra_refs, ket_refs = refs[:groups], refs[groups : groups + early]
         total_ref, last_ref, chosen = refs[groups + early :]
+        chosen[...] = jnp.zeros_like(chosen)
         for d in range(groups):
 
             def put(s, _, d=d):
@@ -135,16 +135,6 @@
                 return 0
 
             lax.fori_loop(0, slots, put, 0, unroll=8)
-
-        def clear(row, _):
-            @pl.when(bra_of_ref[row] < 0)
-            def _():
-                for c in range(2):
-                    chosen[c, row] = jnp.zeros((part, bands), jnp.bfloat16)
-
-            return 0
-
-        lax.fori_loop(0, groups * slots, clear, 0, unroll=8)
         for d in range(early):
             product = jnp.dot(turned(chosen, d), flat(ket_refs[d]), preferred_element_type=jnp.float32)
             if d == 0:
@@ -153,20 +143,23 @@
                 total_ref[...] += product
         last_ref[...] = turned(chosen, early)
 
-    def rest(me_ref, total_ref, last_ref, ket_ref, give_ref, keep_ref, sums):
+    plan = halving_plan(groups)
+
+    def rest(me_ref, total_ref, last_ref, ket_ref, *refs):
+        outs, sums = refs[:-1], refs[-1]
         sums[...] = total_ref[...] + jnp.dot(
             last_ref[...], flat(ket_ref), preferred_element_type=jnp.float32
         )
-        for d in range(groups):
-            out = give_ref if d % 2 else keep_ref
-            start = (me_ref[0] ^ d) * rows
-            for c in range(2):
-                out[d // 2, c] = sums[pl.ds(pl.multiple_of(c * bands + start, rows), rows)] * scale
+        for c in range(2):
+            for out, blocks in zip(outs[2 * c : 2 * c + 2], plan[c][0]):
+                for place, d in enumerate(blocks):
+                    start = c * bands + (me_ref[0] ^ d) * rows
+                    out[place] = sums[pl.ds(pl.multiple_of(start, rows), rows)] * scale
 
     flops = 8 * depth * bands * bands
     total, last = pl.pallas_call(
         most,
-        in_specs=[scalar, scalar] + [near] * (groups + early),
+        in_specs=[scalar] + [near] * (groups + early),
         out_specs=[near, near],
         out_shape=[
             jax.ShapeDtypeStruct((2 * bands, bands), jnp.float32),
@@ -175,17 +168,80 @@
         scratch_shapes=[pltpu.VMEM((2, groups * slots + 1, part, bands), jnp.bfloat16)],
         compiler_params=pltpu.CompilerParams(vmem_limit_bytes=32 << 20),
         cost_estimate=pl.CostEstimate(flops=early * flops, bytes_accessed=1 << 20, transcendentals=0),
-    )(ket_of, bra_of, *bras, *kets[:early])
-    half = jax.ShapeDtypeStruct((groups // 2, 2, rows, bands), jnp.float32)
+    )(ket_of, *bras, *kets[:early])
+    half = jax.ShapeDtypeStruct((groups // 2, rows, bands), jnp.float32)
     return pl.pallas_call(
         rest,
         in_specs=[scalar, near, near, near],
-        out_specs=[near, near],
-        out_shape=[half, half],
+        out_specs=[near] * 4,
+        out_shape=[half] * 4,
         scratch_shapes=[pltpu.VMEM((2 * bands, bands), jnp.float32)],
         compiler_params=pltpu.CompilerParams(vmem_limit_bytes=16 << 20),
         cost_estimate=pl.CostEstimate(flops=flops, bytes_accessed=1 << 20, transcendentals=0),
     )(me.reshape(1), total, last, kets[early])
+
+
+def halving_plan(groups):
+    bits = groups.bit_length() - 1
+    plans = []
+    for order in ([*range(bits)], [1, 0, *range(2, bits)]):
+        blocks, steps = list(range(groups)), []
+        for bit in order:
+            kept = [i for i in blocks if not i >> bit & 1]
+            steps.append(([i | 1 << bit for i in kept], kept))
+            blocks = kept
+        plans.append((steps[0], order, steps))
+    return plans
+
+
+def reduce_to_owner(parts, groups):
+    plan = halving_plan(groups)
+    gives, keeps = [parts[0], parts[2]], [parts[1], parts[3]]
+    _, rows, bands = gives[0].shape
+    steps = groups.bit_length() - 1
+    near = pl.BlockSpec(memory_space=pltpu.VMEM)
+    for step in range(steps):
+        bits = [plan[c][1][step] for c in range(2)]
+        if bits[0] == bits[1] and len(gives) == 1:
+            got = [swapped_with(gives[0], 1 << bits[0])]
+        else:
+            got = [swapped_with(gives[c], 1 << bits[c]) for c in range(2)]
+        if step == steps - 1:
+            break
+        joined = plan[0][1][step + 1] == plan[1][1][step + 1]
+        count = groups >> (step + 2)
+
+        def body(*refs, step=step, joined=joined, count=count, number=len(got)):
+            held, come, outs = refs[:number], refs[number : 2 * number], refs[2 * number :]
+            for c in range(2):
+                steps_of = plan[c][2]
+                now = steps_of[step][1]
+                for kind in range(2):
+                    for place, block in enumerate(steps_of[step + 1][kind]):
+                        at = now.index(block)
+                        source = (c, at) if number == 1 else (at,)
+                        which = 0 if number == 1 else c
+                        value = held[which][source] + come[which][source]
+                        if joined:
+                            outs[kind][c, place] = value
+                        else:
+                            outs[2 * c + kind][place] = value
+
+        if joined:
+            shapes = [jax.ShapeDtypeStruct((2, count, rows, bands), jnp.float32)] * 2
+        else:
+            shapes = [jax.ShapeDtypeStruct((count, rows, bands), jnp.float32)] * 4
+        outs = pl.pallas_call(
+            body,
+            in_specs=[near] * (2 * len(got)),
+            out_specs=[near] * len(shapes),
+            out_shape=shapes,
+            compiler_params=pltpu.CompilerParams(vmem_limit_bytes=8 << 20),
+        )(*keeps, *got)
+        gives, keeps = outs[0::2], outs[1::2]
+    if len(keeps) == 1:
+        return (keeps[0] + got[0])[:, 0]
+    return jnp.stack([(keep + come)[0] for keep, come in zip(keeps, got)])
 
 
 def zero_like(value):
@@ -205,14 +261,14 @@
 def local(coefficients, stick_count, dest_device, dest_slot, source_stick):
     groups = lax.axis_size("ga")
     me = lax.axis_index("ga").astype(jnp.int32)
-    _, slots, _, bands, waves = coefficients.shape
+    _, slots, _, _, waves = coefficients.shape
     scale = (2 * groups * slots * waves) ** (-0.5)
     pieces = pack(coefficients[0], groups, me)
     mine = jnp.concatenate([stick_count, dest_device, dest_slot, source_stick], axis=1)[0]
     info = passed_around(mine, groups)
     bras, kets = [None] * groups, [None] * groups
     bras[0] = pieces[0]
-    arrivals = interleaved(range(1, groups // 2), range(groups // 2, groups))
+    arrivals = arrival_order(groups)
     kets[0] = to_previous_pool(bras[0])
     anchor = me.reshape(1, 1)
     for place, d in enumerate(arrivals):
@@ -223,30 +279,20 @@
         anchor = zero_like(anchor)
         if place == len(arrivals) - 2:
             before_last = anchor
-        if place == groups // 2:
-            even = jnp.stack(info) + anchor
-    odd = swapped_with(even, 1)
-    bra_info = jnp.stack([even, odd], axis=1).reshape(groups, mine.shape[0])
+        if place == 2:
+            bra_info = jnp.stack(info) + anchor
     ket_info = to_previous_pool(bra_info)
-    ket_of, bra_of = pair_lists(bra_info, ket_info + before_last, groups, slots, me)
+    ket_of = pair_list(bra_info, ket_info + before_last, groups, slots, me)
     if (waves // groups) % 16:
-        give, keep = multiply_plainly(bras, kets, ket_of, me, groups, scale)
+        parts = multiply_plainly(bras, kets, ket_of, me, groups, scale)
     else:
-        give, keep = multiply(bras, kets, ket_of, bra_of, me, groups, scale)
-    distance = 1
-    while True:
-        keep = keep + swapped_with(give, distance)
-        distance *= 2
-        if distance == groups:
-            break
-        give, keep = keep[1::2], keep[0::2]
-    return keep.reshape(1, 2, bands // groups, bands)
-
-
-def interleaved(first, second):
-    first, second = list(first), list(second)
-    mixed = [item for pair in zip(first, second) for item in pair]
-    return mixed + second[len(first) :]
+        parts = multiply(bras, kets, ket_of, me, groups, scale)
+    return reduce_to_owner(parts, groups)[None]
+
+
+def arrival_order(groups):
+    near = list(range(1, groups // 2))
+    return [*near[:-1], groups // 2, near[-1], *range(groups // 2 + 1, groups)]
 
 
 def solution(mesh):

time: 163 us -> 163 us (level)
  the two profiles are of different devices: /device:TPU:1 before, /device:TPU:0 now
where the time goes in v3:
time: 163 us
  waiting for transfers between devices  92.4 us (57%)
  starting transfers between devices  45.7 us (28%)
  Pallas kernels  17.8 us (11%)
  other arithmetic  3.03 us (2%)
  local copies, waits for them, and re-layouts  2.98 us (2%)
    ppermute x19, waiting for transfers between devices, swapped_with(): return lax.ppermute(value, 'ga', [(i, i ^ distance) for i in range(count)])  70.7 us
    ppermute x19, starting transfers between devices, swapped_with(): return lax.ppermute(value, 'ga', [(i, i ^ distance) for i in range(count)])  39.7 us
    ppermute x9, waiting for transfers between devices, to_previous_pool(): lax.ppermute(value, 'pool', [(i, (i - 1) % count) for i in range(count)])  21.7 us
    pallas_call x6, Pallas kernels, zero_like(): pl.pallas_call(body, in_specs=[scalar], out_specs=scalar, out_shape=jax.S...  6.08 us
    ppermute x9, starting transfers between devices, to_previous_pool(): lax.ppermute(value, 'pool', [(i, (i - 1) % count) for i in range(count)])  6.05 us
    pallas_call x1, Pallas kernels, multiply(): pl.pallas_call(most, in_specs=[scalar] + [near] * (groups + early), out_s...  5.38 us
    pallas_call x1, Pallas kernels, pack(): pl.pallas_call(body, in_specs=[near, pl.BlockSpec(memory_space=pltpu.HBM)...  4.8 us
  transfers between devices with their start and end apart: 28, of which 16 were waited for; matrix products, arithmetic and copies ran while one was open for 1% of the time, Pallas kernels for 10%

profile of v3, /device:TPU:0, one launch (start us, length us, event | category | flops | bytes accessed | tf_op | source)
XLA Modules:
  0.0 162.8 jit_solution(17532347202536736246)
XLA Ops:
  1.4 3.0 %collective-permute-start = (s32[97]{0:T(128)S(1)}, s32[97]{0:T(128)S(1)}, u32[]{:S(2)}, u32[]{:S(2)}) collective-permute-start(s32[97]{0:T(128)S(1)} %bitcast.16), channel_id=1, source_target_pairs={{0,1},{1,0},{2,3},{3,2},{4,5},{5,4},{6,7},{7,6},{8,9},{9,8},{10,11... | collective-permute-start | bytes 1172 | tf_op jit(solution)/shard_map/ppermute | solution.py:11
  4.4 1.6 collective-permute-start.1
  6.0 3.0 %collective-permute-start.3 = (s32[97]{0:T(128)S(1)}, s32[97]{0:T(128)S(1)}, u32[]{:S(2)}, u32[]{:S(2)}) collective-permute-start(s32[97]{0:T(128)S(1)} %bitcast.19), channel_id=1, source_target_pairs={{0,4},{1,5},{2,6},{3,7},{4,0},{5,1},{6,2},{7,3},{8,12},{9,13},{10,... | collective-permute-start | bytes 1172 | tf_op jit(solution)/shard_map/ppermute | solution.py:11
  9.0 1.3 collective-permute-start.4
  10.3 4.8 %shard_map.61 = (bf16[2,32,16,256]{3,2,1,0:T(8,128)(2,1)S(1)}, bf16[2,32,16,256]{3,2,1,0:T(8,128)(2,1)}, bf16[2,32,16,256]{3,2,1,0:T(8,128)(2,1)}, bf16[2,32,16,...) custom-call(bf16[128,128]{1,0:T(8,128)(2,1)S(1)} %fusion.select_ref,, ...), custom_call_target="tpu_custom_call" | custom-call | flops 536870912 | bytes 8388608 | tf_op jit(solution)/shard_map/pallas_call | solution.py:54
  19.1 1.2 shard_map.57._
  20.3 3.7 %collective-permute-start.5 = (s32[97]{0:T(128)S(1)}, s32[97]{0:T(128)S(1)}, u32[]{:S(2)}, u32[]{:S(2)}) collective-permute-start(s32[97]{0:T(128)S(1)} %bitcast.21), channel_id=1, source_target_pairs={{0,6},{1,7},{2,4},{3,5},{4,2},{5,3},{6,0},{7,1},{8,14},{9,15},{10,... | collective-permute-start | bytes 1172 | tf_op jit(solution)/shard_map/ppermute | solution.py:11
  24.1 1.6 %collective-permute-start.8 = (bf16[2,32,16,256]{3,2,1,0:T(8,128)(2,1)}, bf16[2,32,16,256]{3,2,1,0:T(8,128)(2,1)S(1)}, u32[]{:S(2)}, u32[]{:S(2)}) collective-permute-start(bf16[2,32,16,256]{3,2,1,0:T(8,128)(2,1)} %get-tuple-element.26), channel_id=1, source_target_pairs={{0,1},{1,0},{2,3},{3,2},{4,5},{5,4},{6,7},{7,6},{8,9},{9,8},{10,11... | collective-permute-start | bytes 1572872 | tf_op jit(solution)/shard_map/ppermute | solution.py:11
  25.7 1.9 %collective-permute-start.10 = (bf16[2,32,16,256]{3,2,1,0:T(8,128)(2,1)}, bf16[2,32,16,256]{3,2,1,0:T(8,128)(2,1)S(1)}, u32[]{:S(2)}, u32[]{:S(2)}) collective-permute-start(bf16[2,32,16,256]{3,2,1,0:T(8,128)(2,1)} %get-tuple-element.28), channel_id=1, source_target_pairs={{0,3},{1,2},{2,1},{3,0},{4,7},{5,6},{6,5},{7,4},{8,11},{9,10},{10,... | collective-permute-start | bytes 1572872 | tf_op jit(solution)/shard_map/ppermute | solution.py:11
  27.6 2.4 %collective-permute-start.11 = (bf16[2,32,16,256]{3,2,1,0:T(8,128)(2,1)}, bf16[2,32,16,256]{3,2,1,0:T(8,128)(2,1)S(1)}, u32[]{:S(2)}, u32[]{:S(2)}) collective-permute-start(bf16[2,32,16,256]{3,2,1,0:T(8,128)(2,1)} %get-tuple-element.29), channel_id=1, source_target_pairs={{0,4},{1,5},{2,6},{3,7},{4,0},{5,1},{6,2},{7,3},{8,12},{9,13},{10,... | collective-permute-start | bytes 1572872 | tf_op jit(solution)/shard_map/ppermute | solution.py:11
  31.0 1.3 collective-permute-done.7
  33.5 2.8 %collective-permute-done.8.refs_1_ = bf16[2,32,16,256]{3,2,1,0:T(8,128)(2,1)S(1)} collective-permute-done((bf16[2,32,16,256]{3,2,1,0:T(8,128)(2,1)}, bf16[2,32,16,256]{3,2,1,0:T(8,128)(2,1)S(1)}, u32[]{:S(2)}, u32[]{:S(2)}) %collective-permute-start.8) | collective-permute-done | bytes 524320 | tf_op jit(solution)/shard_map/ppermute | solution.py:11
  36.3 3.4 %collective-permute-start.13 = (bf16[2,32,16,256]{3,2,1,0:T(8,128)(2,1)}, bf16[2,32,16,256]{3,2,1,0:T(8,128)(2,1)}, u32[]{:S(2)}, u32[]{:S(2)}) collective-permute-start(bf16[2,32,16,256]{3,2,1,0:T(8,128)(2,1)} %copy-done.1), channel_id=1, source_target_pairs={{0,6},{1,7},{2,4},{3,5},{4,2},{5,3},{6,0},{7,1},{8,14},{9,15},{10,... | collective-permute-start | bytes 1572872 | tf_op jit(solution)/shard_map/ppermute | solution.py:11
  39.7 21.6 %collective-permute-done.9.refs_2_ = bf16[2,32,16,256]{3,2,1,0:T(8,128)(2,1)S(1)} collective-permute-done((bf16[2,32,16,256]{3,2,1,0:T(8,128)(2,1)}, bf16[2,32,16,256]{3,2,1,0:T(8,128)(2,1)S(1)}, u32[]{:S(2)}, u32[]{:S(2)}) %collective-permute-start.9) | collective-permute-done | bytes 524320 | tf_op jit(solution)/shard_map/ppermute | solution.py:11
  62.1 7.3 %collective-permute-done.10.refs_3_ = bf16[2,32,16,256]{3,2,1,0:T(8,128)(2,1)S(1)} collective-permute-done((bf16[2,32,16,256]{3,2,1,0:T(8,128)(2,1)}, bf16[2,32,16,256]{3,2,1,0:T(8,128)(2,1)S(1)}, u32[]{:S(2)}, u32[]{:S(2)}) %collective-permute-start.10) | collective-permute-done | bytes 524320 | tf_op jit(solution)/shard_map/ppermute | solution.py:11
  70.6 28.4 %collective-permute-done.12.refs_5_ = bf16[2,32,16,256]{3,2,1,0:T(8,128)(2,1)S(1)} collective-permute-done((bf16[2,32,16,256]{3,2,1,0:T(8,128)(2,1)}, bf16[2,32,16,256]{3,2,1,0:T(8,128)(2,1)S(1)}, u32[]{:S(2)}, u32[]{:S(2)}) %collective-permute-start.12) | collective-permute-done | bytes 524320 | tf_op jit(solution)/shard_map/ppermute | solution.py:11
  102.6 2.6 %collective-permute-start.18 = (bf16[2,32,16,256]{3,2,1,0:T(8,128)(2,1)S(1)}, bf16[2,32,16,256]{3,2,1,0:T(8,128)(2,1)}, u32[]{:S(2)}, u32[]{:S(2)}) collective-permute-start(bf16[2,32,16,256]{3,2,1,0:T(8,128)(2,1)S(1)} %collective-permute-done.10.refs_3_), channel_id=1, source_target_pairs={{0,24},{8,0},{16,8},{24,16},{1,25},{9,1},{17,9},{25,17},{2,26},{10... | collective-permute-start | bytes 1572872 | tf_op jit(solution)/shard_map/ppermute | solution.py:16
  105.6 2.0 %collective-permute-start.22 = (bf16[2,32,16,256]{3,2,1,0:T(8,128)(2,1)}, bf16[2,32,16,256]{3,2,1,0:T(8,128)(2,1)}, u32[]{:S(2)}, u32[]{:S(2)}) collective-permute-start(bf16[2,32,16,256]{3,2,1,0:T(8,128)(2,1)} %collective-permute-done.14.refs_7_), channel_id=1, source_target_pairs={{0,24},{8,0},{16,8},{24,16},{1,25},{9,1},{17,9},{25,17},{2,26},{10... | collective-permute-start | bytes 1572872 | tf_op jit(solution)/shard_map/ppermute | solution.py:16
  109.0 3.0 %collective-permute-done.18.refs_11_ = bf16[2,32,16,256]{3,2,1,0:T(8,128)(2,1)} collective-permute-done((bf16[2,32,16,256]{3,2,1,0:T(8,128)(2,1)S(1)}, bf16[2,32,16,256]{3,2,1,0:T(8,128)(2,1)}, u32[]{:S(2)}, u32[]{:S(2)}) %collective-permute-start.18) | collective-permute-done | bytes 524320 | tf_op jit(solution)/shard_map/ppermute | solution.py:16
  111.9 5.6 %collective-permute-done.19.refs_12_ = bf16[2,32,16,256]{3,2,1,0:T(8,128)(2,1)} collective-permute-done((bf16[2,32,16,256]{3,2,1,0:T(8,128)(2,1)S(1)}, bf16[2,32,16,256]{3,2,1,0:T(8,128)(2,1)}, u32[]{:S(2)}, u32[]{:S(2)}) %collective-permute-start.19) | collective-permute-done | bytes 524320 | tf_op jit(solution)/shard_map/ppermute | solution.py:16
  117.5 5.6 %collective-permute-done.20.refs_13_ = bf16[2,32,16,256]{3,2,1,0:T(8,128)(2,1)} collective-permute-done((bf16[2,32,16,256]{3,2,1,0:T(8,128)(2,1)S(1)}, bf16[2,32,16,256]{3,2,1,0:T(8,128)(2,1)}, u32[]{:S(2)}, u32[]{:S(2)}) %collective-permute-start.20) | collective-permute-done | bytes 524320 | tf_op jit(solution)/shard_map/ppermute | solution.py:16
  123.1 5.7 %collective-permute-done.21.refs_14_ = bf16[2,32,16,256]{3,2,1,0:T(8,128)(2,1)} collective-permute-done((bf16[2,32,16,256]{3,2,1,0:T(8,128)(2,1)}, bf16[2,32,16,256]{3,2,1,0:T(8,128)(2,1)}, u32[]{:S(2)}, u32[]{:S(2)}) %collective-permute-start.21) | collective-permute-done | bytes 524320 | tf_op jit(solution)/shard_map/ppermute | solution.py:16
  128.9 5.4 %shard_map.62 = (f32[512,256]{1,0:T(8,128)S(1)}, bf16[512,1024]{1,0:T(8,128)(2,1)S(1)}) custom-call(s32[256]{0:T(256)S(1)} %select_reduce_fusion.ket_of_ref, bf16[2,32,16,256]{3,2,1,0:T(8,128)(2,1)S(1)} %get-tuple-element.25.refs_0_, bf16[2,32,16,256]{3,2,1,0:T(8,128)(2,1)S(1)} %collective-permute-done.8.refs_1_, ...), custom_call_target="tpu_custom_call" | custom-call | flops 1879048192 | bytes 1048576 | tf_op jit(solution)/shard_map/pallas_call | solution.py:160
  134.5 1.5 shard_map.63
  136.1 9.9 %collective-permute-start.24 = (f32[4,32,256]{2,1,0:T(8,128)S(1)}, f32[4,32,256]{2,1,0:T(8,128)S(1)}, u32[]{:S(2)}, u32[]{:S(2)}) collective-permute-start(f32[4,32,256]{2,1,0:T(8,128)S(1)} %get-tuple-element.38), channel_id=1, source_target_pairs={{0,2},{1,3},{2,0},{3,1},{4,6},{5,7},{6,4},{7,5},{8,10},{9,11},{10,... | collective-permute-start | bytes 393224 | tf_op jit(solution)/shard_map/ppermute | solution.py:11
  146.0 3.5 %collective-permute-done.24.refs_3_ = f32[4,32,256]{2,1,0:T(8,128)S(1)} collective-permute-done((f32[4,32,256]{2,1,0:T(8,128)S(1)}, f32[4,32,256]{2,1,0:T(8,128)S(1)}, u32[]{:S(2)}, u32[]{:S(2)}) %collective-permute-start.24) | collective-permute-done | bytes 131104 | tf_op jit(solution)/shard_map/ppermute | solution.py:11
  149.6 2.4 %collective-permute-start.25 = (f32[2,32,256]{2,1,0:T(8,128)S(1)}, f32[2,32,256]{2,1,0:T(8,128)S(1)}, u32[]{:S(2)}, u32[]{:S(2)}) collective-permute-start(f32[2,32,256]{2,1,0:T(8,128)S(1)} %get-tuple-element.41), channel_id=1, source_target_pairs={{0,2},{1,3},{2,0},{3,1},{4,6},{5,7},{6,4},{7,5},{8,10},{9,11},{10,... | collective-permute-start | bytes 196616 | tf_op jit(solution)/shard_map/ppermute | solution.py:11
  151.9 1.4 collective-permute-start.26
  153.3 1.2 collective-permute-done.25.refs_2_
  154.6 1.6 %collective-permute-done.26.refs_3_ = f32[2,32,256]{2,1,0:T(8,128)S(1)} collective-permute-done((f32[2,32,256]{2,1,0:T(8,128)S(1)}, f32[2,32,256]{2,1,0:T(8,128)S(1)}, u32[]{:S(2)}, u32[]{:S(2)}) %collective-permute-start.26) | collective-permute-done | bytes 65568 | tf_op jit(solution)/shard_map/ppermute | solution.py:11
  156.2 2.1 %collective-permute-start.27 = (f32[2,1,32,256]{3,2,1,0:T(8,128)S(1)}, f32[2,1,32,256]{3,2,1,0:T(8,128)S(1)}, u32[]{:S(2)}, u32[]{:S(2)}) collective-permute-start(f32[2,1,32,256]{3,2,1,0:T(8,128)S(1)} %get-tuple-element.44), channel_id=1, source_target_pairs={{0,4},{1,5},{2,6},{3,7},{4,0},{5,1},{6,2},{7,3},{8,12},{9,13},{10,... | collective-permute-start | bytes 196616 | tf_op jit(solution)/shard_map/ppermute | solution.py:11
  158.4 3.8 %collective-permute-done.27 = f32[2,1,32,256]{3,2,1,0:T(8,128)S(1)} collective-permute-done((f32[2,1,32,256]{3,2,1,0:T(8,128)S(1)}, f32[2,1,32,256]{3,2,1,0:T(8,128)S(1)}, u32[]{:S(2)}, u32[]{:S(2)}) %collective-permute-start.27) | collective-permute-done | bytes 65568 | tf_op jit(solution)/shard_map/ppermute | solution.py:11
  (59 shorter events, 15.4 us)
Async XLA Ops:
  1.4 18.9 %collective-permute-start = (s32[97]{0:T(128)S(1)}, s32[97]{0:T(128)S(1)}, u32[]{:S(2)}, u32[]{:S(2)}) collective-permute-start(s32[97]{0:T(128)S(1)} %bitcast.16), channel_id=1, source_target_pairs={{0,1},{1,0},{2,3},{3,2},{4,5},{5,4},{6,7},{7,6},{8,9},{9,8},{10,11... | collective-permute-start | bytes 1172 | tf_op jit(solution)/shard_map/ppermute | solution.py:11
  4.4 19.6 %collective-permute-start.1 = (s32[97]{0:T(128)S(1)}, s32[97]{0:T(128)S(1)}, u32[]{:S(2)}, u32[]{:S(2)}) collective-permute-start(s32[97]{0:T(128)S(1)} %bitcast.17), channel_id=1, source_target_pairs={{0,2},{1,3},{2,0},{3,1},{4,6},{5,7},{6,4},{7,5},{8,10},{9,11},{10,... | collective-permute-start | bytes 1172 | tf_op jit(solution)/shard_map/ppermute | solution.py:11
  6.0 18.1 %collective-permute-start.2 = (s32[97]{0:T(128)S(1)}, s32[97]{0:T(128)S(1)}, u32[]{:S(2)}, u32[]{:S(2)}) collective-permute-start(s32[97]{0:T(128)S(1)} %bitcast.18), channel_id=1, source_target_pairs={{0,3},{1,2},{2,1},{3,0},{4,7},{5,6},{6,5},{7,4},{8,11},{9,10},{10,... | collective-permute-start | bytes 1172 | tf_op jit(solution)/shard_map/ppermute | solution.py:11
  6.0 19.7 %collective-permute-start.3 = (s32[97]{0:T(128)S(1)}, s32[97]{0:T(128)S(1)}, u32[]{:S(2)}, u32[]{:S(2)}) collective-permute-start(s32[97]{0:T(128)S(1)} %bitcast.19), channel_id=1, source_target_pairs={{0,4},{1,5},{2,6},{3,7},{4,0},{5,1},{6,2},{7,3},{8,12},{9,13},{10,... | collective-permute-start | bytes 1172 | tf_op jit(solution)/shard_map/ppermute | solution.py:11
  9.0 16.7 %collective-permute-start.4 = (s32[97]{0:T(128)S(1)}, s32[97]{0:T(128)S(1)}, u32[]{:S(2)}, u32[]{:S(2)}) collective-permute-start(s32[97]{0:T(128)S(1)} %bitcast.20), channel_id=1, source_target_pairs={{0,5},{1,4},{2,7},{3,6},{4,1},{5,0},{6,3},{7,2},{8,13},{9,12},{10,... | collective-permute-start | bytes 1172 | tf_op jit(solution)/shard_map/ppermute | solution.py:11
  15.1 0.8 copy-start
  15.9 0.8 copy-start.1
  16.8 0.8 copy-start.2
  20.3 7.2 %collective-permute-start.5 = (s32[97]{0:T(128)S(1)}, s32[97]{0:T(128)S(1)}, u32[]{:S(2)}, u32[]{:S(2)}) collective-permute-start(s32[97]{0:T(128)S(1)} %bitcast.21), channel_id=1, source_target_pairs={{0,6},{1,7},{2,4},{3,5},{4,2},{5,3},{6,0},{7,1},{8,14},{9,15},{10,... | collective-permute-start | bytes 1172 | tf_op jit(solution)/shard_map/ppermute | solution.py:11
  24.0 6.4 %collective-permute-start.6 = (s32[97]{0:T(128)S(1)}, s32[97]{0:T(128)S(1)}, u32[]{:S(2)}, u32[]{:S(2)}) collective-permute-start(s32[97]{0:T(128)S(1)} %bitcast.22), channel_id=1, source_target_pairs={{0,7},{1,6},{2,5},{3,4},{4,3},{5,2},{6,1},{7,0},{8,15},{9,14},{10,... | collective-permute-start | bytes 1172 | tf_op jit(solution)/shard_map/ppermute | solution.py:11
  24.1 12.2 %collective-permute-start.8 = (bf16[2,32,16,256]{3,2,1,0:T(8,128)(2,1)}, bf16[2,32,16,256]{3,2,1,0:T(8,128)(2,1)S(1)}, u32[]{:S(2)}, u32[]{:S(2)}) collective-permute-start(bf16[2,32,16,256]{3,2,1,0:T(8,128)(2,1)} %get-tuple-element.26), channel_id=1, source_target_pairs={{0,1},{1,0},{2,3},{3,2},{4,5},{5,4},{6,7},{7,6},{8,9},{9,8},{10,11... | collective-permute-start | bytes 1572872 | tf_op jit(solution)/shard_map/ppermute | solution.py:11
  25.7 35.7 %collective-permute-start.9 = (bf16[2,32,16,256]{3,2,1,0:T(8,128)(2,1)}, bf16[2,32,16,256]{3,2,1,0:T(8,128)(2,1)S(1)}, u32[]{:S(2)}, u32[]{:S(2)}) collective-permute-start(bf16[2,32,16,256]{3,2,1,0:T(8,128)(2,1)} %get-tuple-element.27), channel_id=1, source_target_pairs={{0,2},{1,3},{2,0},{3,1},{4,6},{5,7},{6,4},{7,5},{8,10},{9,11},{10,... | collective-permute-start | bytes 1572872 | tf_op jit(solution)/shard_map/ppermute | solution.py:11
  25.7 43.7 %collective-permute-start.10 = (bf16[2,32,16,256]{3,2,1,0:T(8,128)(2,1)}, bf16[2,32,16,256]{3,2,1,0:T(8,128)(2,1)S(1)}, u32[]{:S(2)}, u32[]{:S(2)}) collective-permute-start(bf16[2,32,16,256]{3,2,1,0:T(8,128)(2,1)} %get-tuple-element.28), channel_id=1, source_target_pairs={{0,3},{1,2},{2,1},{3,0},{4,7},{5,6},{6,5},{7,4},{8,11},{9,10},{10,... | collective-permute-start | bytes 1572872 | tf_op jit(solution)/shard_map/ppermute | solution.py:11
  27.6 41.9 %collective-permute-start.11 = (bf16[2,32,16,256]{3,2,1,0:T(8,128)(2,1)}, bf16[2,32,16,256]{3,2,1,0:T(8,128)(2,1)S(1)}, u32[]{:S(2)}, u32[]{:S(2)}) collective-permute-start(bf16[2,32,16,256]{3,2,1,0:T(8,128)(2,1)} %get-tuple-element.29), channel_id=1, source_target_pairs={{0,4},{1,5},{2,6},{3,7},{4,0},{5,1},{6,2},{7,3},{8,12},{9,13},{10,... | collective-permute-start | bytes 1572872 | tf_op jit(solution)/shard_map/ppermute | solution.py:11
  31.0 1.4 collective-permute-start.7
  32.4 66.6 %collective-permute-start.12 = (bf16[2,32,16,256]{3,2,1,0:T(8,128)(2,1)}, bf16[2,32,16,256]{3,2,1,0:T(8,128)(2,1)S(1)}, u32[]{:S(2)}, u32[]{:S(2)}) collective-permute-start(bf16[2,32,16,256]{3,2,1,0:T(8,128)(2,1)} %copy-done.2), channel_id=1, source_target_pairs={{0,5},{1,4},{2,7},{3,6},{4,1},{5,0},{6,3},{7,2},{8,13},{9,12},{10,... | collective-permute-start | bytes 1572872 | tf_op jit(solution)/shard_map/ppermute | solution.py:11
  36.3 66.3 %collective-permute-start.13 = (bf16[2,32,16,256]{3,2,1,0:T(8,128)(2,1)}, bf16[2,32,16,256]{3,2,1,0:T(8,128)(2,1)}, u32[]{:S(2)}, u32[]{:S(2)}) collective-permute-start(bf16[2,32,16,256]{3,2,1,0:T(8,128)(2,1)} %copy-done.1), channel_id=1, source_target_pairs={{0,6},{1,7},{2,4},{3,5},{4,2},{5,3},{6,0},{7,1},{8,14},{9,15},{10,... | collective-permute-start | bytes 1572872 | tf_op jit(solution)/shard_map/ppermute | solution.py:11
  61.4 43.8 %collective-permute-start.14 = (bf16[2,32,16,256]{3,2,1,0:T(8,128)(2,1)}, bf16[2,32,16,256]{3,2,1,0:T(8,128)(2,1)}, u32[]{:S(2)}, u32[]{:S(2)}) collective-permute-start(bf16[2,32,16,256]{3,2,1,0:T(8,128)(2,1)} %copy-done), channel_id=1, source_target_pairs={{0,7},{1,6},{2,5},{3,4},{4,3},{5,2},{6,1},{7,0},{8,15},{9,14},{10,... | collective-permute-start | bytes 1572872 | tf_op jit(solution)/shard_map/ppermute | solution.py:11
  69.4 35.8 %collective-permute-start.15 = (bf16[2,32,16,256]{3,2,1,0:T(8,128)(2,1)S(1)}, bf16[2,32,16,256]{3,2,1,0:T(8,128)(2,1)}, u32[]{:S(2)}, u32[]{:S(2)}) collective-permute-start(bf16[2,32,16,256]{3,2,1,0:T(8,128)(2,1)S(1)} %get-tuple-element.25.refs_0_), channel_id=1, source_target_pairs={{0,24},{8,0},{16,8},{24,16},{1,25},{9,1},{17,9},{25,17},{2,26},{10... | collective-permute-start | bytes 1572872 | tf_op jit(solution)/shard_map/ppermute | solution.py:16
  69.4 35.9 %collective-permute-start.16 = (bf16[2,32,16,256]{3,2,1,0:T(8,128)(2,1)S(1)}, bf16[2,32,16,256]{3,2,1,0:T(8,128)(2,1)}, u32[]{:S(2)}, u32[]{:S(2)}) collective-permute-start(bf16[2,32,16,256]{3,2,1,0:T(8,128)(2,1)S(1)} %collective-permute-done.8.refs_1_), channel_id=1, source_target_pairs={{0,24},{8,0},{16,8},{24,16},{1,25},{9,1},{17,9},{25,17},{2,26},{10... | collective-permute-start | bytes 1572872 | tf_op jit(solution)/shard_map/ppermute | solution.py:16
  98.9 6.7 %collective-permute-start.17 = (bf16[2,32,16,256]{3,2,1,0:T(8,128)(2,1)S(1)}, bf16[2,32,16,256]{3,2,1,0:T(8,128)(2,1)}, u32[]{:S(2)}, u32[]{:S(2)}) collective-permute-start(bf16[2,32,16,256]{3,2,1,0:T(8,128)(2,1)S(1)} %collective-permute-done.9.refs_2_), channel_id=1, source_target_pairs={{0,24},{8,0},{16,8},{24,16},{1,25},{9,1},{17,9},{25,17},{2,26},{10... | collective-permute-start | bytes 1572872 | tf_op jit(solution)/shard_map/ppermute | solution.py:16
  102.6 9.3 %collective-permute-start.18 = (bf16[2,32,16,256]{3,2,1,0:T(8,128)(2,1)S(1)}, bf16[2,32,16,256]{3,2,1,0:T(8,128)(2,1)}, u32[]{:S(2)}, u32[]{:S(2)}) collective-permute-start(bf16[2,32,16,256]{3,2,1,0:T(8,128)(2,1)S(1)} %collective-permute-done.10.refs_3_), channel_id=1, source_target_pairs={{0,24},{8,0},{16,8},{24,16},{1,25},{9,1},{17,9},{25,17},{2,26},{10... | collective-permute-start | bytes 1572872 | tf_op jit(solution)/shard_map/ppermute | solution.py:16
  105.2 12.3 %collective-permute-start.19 = (bf16[2,32,16,256]{3,2,1,0:T(8,128)(2,1)S(1)}, bf16[2,32,16,256]{3,2,1,0:T(8,128)(2,1)}, u32[]{:S(2)}, u32[]{:S(2)}) collective-permute-start(bf16[2,32,16,256]{3,2,1,0:T(8,128)(2,1)S(1)} %collective-permute-done.11.refs_4_), channel_id=1, source_target_pairs={{0,24},{8,0},{16,8},{24,16},{1,25},{9,1},{17,9},{25,17},{2,26},{10... | collective-permute-start | bytes 1572872 | tf_op jit(solution)/shard_map/ppermute | solution.py:16
  105.3 17.9 %collective-permute-start.20 = (bf16[2,32,16,256]{3,2,1,0:T(8,128)(2,1)S(1)}, bf16[2,32,16,256]{3,2,1,0:T(8,128)(2,1)}, u32[]{:S(2)}, u32[]{:S(2)}) collective-permute-start(bf16[2,32,16,256]{3,2,1,0:T(8,128)(2,1)S(1)} %collective-permute-done.12.refs_5_), channel_id=1, source_target_pairs={{0,24},{8,0},{16,8},{24,16},{1,25},{9,1},{17,9},{25,17},{2,26},{10... | collective-permute-start | bytes 1572872 | tf_op jit(solution)/shard_map/ppermute | solution.py:16
  105.4 23.5 %collective-permute-start.21 = (bf16[2,32,16,256]{3,2,1,0:T(8,128)(2,1)}, bf16[2,32,16,256]{3,2,1,0:T(8,128)(2,1)}, u32[]{:S(2)}, u32[]{:S(2)}) collective-permute-start(bf16[2,32,16,256]{3,2,1,0:T(8,128)(2,1)} %collective-permute-done.13.refs_6_), channel_id=1, source_target_pairs={{0,24},{8,0},{16,8},{24,16},{1,25},{9,1},{17,9},{25,17},{2,26},{10... | collective-permute-start | bytes 1572872 | tf_op jit(solution)/shard_map/ppermute | solution.py:16
  105.6 28.8 %collective-permute-start.22 = (bf16[2,32,16,256]{3,2,1,0:T(8,128)(2,1)}, bf16[2,32,16,256]{3,2,1,0:T(8,128)(2,1)}, u32[]{:S(2)}, u32[]{:S(2)}) collective-permute-start(bf16[2,32,16,256]{3,2,1,0:T(8,128)(2,1)} %collective-permute-done.14.refs_7_), channel_id=1, source_target_pairs={{0,24},{8,0},{16,8},{24,16},{1,25},{9,1},{17,9},{25,17},{2,26},{10... | collective-permute-start | bytes 1572872 | tf_op jit(solution)/shard_map/ppermute | solution.py:16
  136.0 10.0 %collective-permute-start.23 = (f32[4,32,256]{2,1,0:T(8,128)S(1)}, f32[4,32,256]{2,1,0:T(8,128)S(1)}, u32[]{:S(2)}, u32[]{:S(2)}) collective-permute-start(f32[4,32,256]{2,1,0:T(8,128)S(1)} %get-tuple-element.37), channel_id=1, source_target_pairs={{0,1},{1,0},{2,3},{3,2},{4,5},{5,4},{6,7},{7,6},{8,9},{9,8},{10,11... | collective-permute-start | bytes 393224 | tf_op jit(solution)/shard_map/ppermute | solution.py:11
  136.1 13.4 %collective-permute-start.24 = (f32[4,32,256]{2,1,0:T(8,128)S(1)}, f32[4,32,256]{2,1,0:T(8,128)S(1)}, u32[]{:S(2)}, u32[]{:S(2)}) collective-permute-start(f32[4,32,256]{2,1,0:T(8,128)S(1)} %get-tuple-element.38), channel_id=1, source_target_pairs={{0,2},{1,3},{2,0},{3,1},{4,6},{5,7},{6,4},{7,5},{8,10},{9,11},{10,... | collective-permute-start | bytes 393224 | tf_op jit(solution)/shard_map/ppermute | solution.py:11
  149.6 5.0 %collective-permute-start.25 = (f32[2,32,256]{2,1,0:T(8,128)S(1)}, f32[2,32,256]{2,1,0:T(8,128)S(1)}, u32[]{:S(2)}, u32[]{:S(2)}) collective-permute-start(f32[2,32,256]{2,1,0:T(8,128)S(1)} %get-tuple-element.41), channel_id=1, source_target_pairs={{0,2},{1,3},{2,0},{3,1},{4,6},{5,7},{6,4},{7,5},{8,10},{9,11},{10,... | collective-permute-start | bytes 196616 | tf_op jit(solution)/shard_map/ppermute | solution.py:11
  151.9 4.3 %collective-permute-start.26 = (f32[2,32,256]{2,1,0:T(8,128)S(1)}, f32[2,32,256]{2,1,0:T(8,128)S(1)}, u32[]{:S(2)}, u32[]{:S(2)}) collective-permute-start(f32[2,32,256]{2,1,0:T(8,128)S(1)} %get-tuple-element.42), channel_id=1, source_target_pairs={{0,1},{1,0},{2,3},{3,2},{4,5},{5,4},{6,7},{7,6},{8,9},{9,8},{10,11... | collective-permute-start | bytes 196616 | tf_op jit(solution)/shard_map/ppermute | solution.py:11
  156.2 5.9 %collective-permute-start.27 = (f32[2,1,32,256]{3,2,1,0:T(8,128)S(1)}, f32[2,1,32,256]{3,2,1,0:T(8,128)S(1)}, u32[]{:S(2)}, u32[]{:S(2)}) collective-permute-start(f32[2,1,32,256]{3,2,1,0:T(8,128)S(1)} %get-tuple-element.44), channel_id=1, source_target_pairs={{0,4},{1,5},{2,6},{3,7},{4,0},{5,1},{6,2},{7,3},{8,12},{9,13},{10,... | collective-permute-start | bytes 196616 | tf_op jit(solution)/shard_map/ppermute | solution.py:11

commit v4 on v3

--- a/solution.py
+++ b/solution.py
@@ -268,7 +268,7 @@
     info = passed_around(mine, groups)
     bras, kets = [None] * groups, [None] * groups
     bras[0] = pieces[0]
-    arrivals = arrival_order(groups)
+    arrivals = range(1, groups)
     kets[0] = to_previous_pool(bras[0])
     anchor = me.reshape(1, 1)
     for place, d in enumerate(arrivals):
@@ -279,7 +279,7 @@
         anchor = zero_like(anchor)
         if place == len(arrivals) - 2:
             before_last = anchor
-        if place == 2:
+        if place == groups // 2 - 1:
             bra_info = jnp.stack(info) + anchor
     ket_info = to_previous_pool(bra_info)
     ket_of = pair_list(bra_info, ket_info + before_last, groups, slots, me)
@@ -288,11 +288,6 @@
     else:
         parts = multiply(bras, kets, ket_of, me, groups, scale)
     return reduce_to_owner(parts, groups)[None]
-
-
-def arrival_order(groups):
-    near = list(range(1, groups // 2))
-    return [*near[:-1], groups // 2, near[-1], *range(groups // 2 + 1, groups)]
 
 
 def solution(mesh):

time: 163 us -> 164 us (level)
  no operation moved by 1% of the time
where the time goes in v4:
time: 164 us
  waiting for transfers between devices  92.8 us (57%)
  starting transfers between devices  46.4 us (28%)
  Pallas kernels  17.9 us (11%)
  other arithmetic  3.03 us (2%)
  local copies, waits for them, and re-layouts  2.98 us (2%)
    ppermute x19, waiting for transfers between devices, swapped_with(): return lax.ppermute(value, 'ga', [(i, i ^ distance) for i in range(count)])  70.7 us
    ppermute x19, starting transfers between devices, swapped_with(): return lax.ppermute(value, 'ga', [(i, i ^ distance) for i in range(count)])  40.3 us
    ppermute x9, waiting for transfers between devices, to_previous_pool(): lax.ppermute(value, 'pool', [(i, (i - 1) % count) for i in range(count)])  22.1 us
    pallas_call x6, Pallas kernels, zero_like(): pl.pallas_call(body, in_specs=[scalar], out_specs=scalar, out_shape=jax.S...  6.21 us
    ppermute x9, starting transfers between devices, to_previous_pool(): lax.ppermute(value, 'pool', [(i, (i - 1) % count) for i in range(count)])  6.05 us
    pallas_call x1, Pallas kernels, multiply(): pl.pallas_call(most, in_specs=[scalar] + [near] * (groups + early), out_s...  5.38 us
    pallas_call x1, Pallas kernels, pack(): pl.pallas_call(body, in_specs=[near, pl.BlockSpec(memory_space=pltpu.HBM)...  4.8 us
  transfers between devices with their start and end apart: 28, of which 16 were waited for; matrix products, arithmetic and copies ran while one was open for 1% of the time, Pallas kernels for 10%

profile of v4, /device:TPU:0, one launch (start us, length us, event | category | flops | bytes accessed | tf_op | source)
XLA Modules:
  0.0 164.0 jit_solution(10346929822033916431)
XLA Ops:
  1.4 3.0 %collective-permute-start = (s32[97]{0:T(128)S(1)}, s32[97]{0:T(128)S(1)}, u32[]{:S(2)}, u32[]{:S(2)}) collective-permute-start(s32[97]{0:T(128)S(1)} %bitcast.16), channel_id=1, source_target_pairs={{0,1},{1,0},{2,3},{3,2},{4,5},{5,4},{6,7},{7,6},{8,9},{9,8},{10,11... | collective-permute-start | bytes 1172 | tf_op jit(solution)/shard_map/ppermute | solution.py:11
  4.4 1.6 collective-permute-start.1
  6.0 3.0 %collective-permute-start.3 = (s32[97]{0:T(128)S(1)}, s32[97]{0:T(128)S(1)}, u32[]{:S(2)}, u32[]{:S(2)}) collective-permute-start(s32[97]{0:T(128)S(1)} %bitcast.19), channel_id=1, source_target_pairs={{0,4},{1,5},{2,6},{3,7},{4,0},{5,1},{6,2},{7,3},{8,12},{9,13},{10,... | collective-permute-start | bytes 1172 | tf_op jit(solution)/shard_map/ppermute | solution.py:11
  9.0 1.3 collective-permute-start.4
  10.3 4.8 %shard_map.61 = (bf16[2,32,16,256]{3,2,1,0:T(8,128)(2,1)S(1)}, bf16[2,32,16,256]{3,2,1,0:T(8,128)(2,1)}, bf16[2,32,16,256]{3,2,1,0:T(8,128)(2,1)}, bf16[2,32,16,...) custom-call(bf16[128,128]{1,0:T(8,128)(2,1)S(1)} %fusion.select_ref,, ...), custom_call_target="tpu_custom_call" | custom-call | flops 536870912 | bytes 8388608 | tf_op jit(solution)/shard_map/pallas_call | solution.py:54
  21.5 3.7 %collective-permute-start.5 = (s32[97]{0:T(128)S(1)}, s32[97]{0:T(128)S(1)}, u32[]{:S(2)}, u32[]{:S(2)}) collective-permute-start(s32[97]{0:T(128)S(1)} %bitcast.21), channel_id=1, source_target_pairs={{0,6},{1,7},{2,4},{3,5},{4,2},{5,3},{6,0},{7,1},{8,14},{9,15},{10,... | collective-permute-start | bytes 1172 | tf_op jit(solution)/shard_map/ppermute | solution.py:11
  25.3 1.6 collective-permute-start.8
  26.9 1.9 %collective-permute-start.10 = (bf16[2,32,16,256]{3,2,1,0:T(8,128)(2,1)}, bf16[2,32,16,256]{3,2,1,0:T(8,128)(2,1)S(1)}, u32[]{:S(2)}, u32[]{:S(2)}) collective-permute-start(bf16[2,32,16,256]{3,2,1,0:T(8,128)(2,1)} %get-tuple-element.28), channel_id=1, source_target_pairs={{0,3},{1,2},{2,1},{3,0},{4,7},{5,6},{6,5},{7,4},{8,11},{9,10},{10,... | collective-permute-start | bytes 1572872 | tf_op jit(solution)/shard_map/ppermute | solution.py:11
  28.8 2.4 %collective-permute-start.11 = (bf16[2,32,16,256]{3,2,1,0:T(8,128)(2,1)}, bf16[2,32,16,256]{3,2,1,0:T(8,128)(2,1)S(1)}, u32[]{:S(2)}, u32[]{:S(2)}) collective-permute-start(bf16[2,32,16,256]{3,2,1,0:T(8,128)(2,1)} %get-tuple-element.29), channel_id=1, source_target_pairs={{0,4},{1,5},{2,6},{3,7},{4,0},{5,1},{6,2},{7,3},{8,12},{9,13},{10,... | collective-permute-start | bytes 1572872 | tf_op jit(solution)/shard_map/ppermute | solution.py:11
  32.2 1.3 collective-permute-done.7
  34.7 2.8 %collective-permute-done.8.refs_1_ = bf16[2,32,16,256]{3,2,1,0:T(8,128)(2,1)S(1)} collective-permute-done((bf16[2,32,16,256]{3,2,1,0:T(8,128)(2,1)}, bf16[2,32,16,256]{3,2,1,0:T(8,128)(2,1)S(1)}, u32[]{:S(2)}, u32[]{:S(2)}) %collective-permute-start.8) | collective-permute-done | bytes 524320 | tf_op jit(solution)/shard_map/ppermute | solution.py:11
  37.5 3.4 %collective-permute-start.13 = (bf16[2,32,16,256]{3,2,1,0:T(8,128)(2,1)}, bf16[2,32,16,256]{3,2,1,0:T(8,128)(2,1)}, u32[]{:S(2)}, u32[]{:S(2)}) collective-permute-start(bf16[2,32,16,256]{3,2,1,0:T(8,128)(2,1)} %copy-done.1), channel_id=1, source_target_pairs={{0,6},{1,7},{2,4},{3,5},{4,2},{5,3},{6,0},{7,1},{8,14},{9,15},{10,... | collective-permute-start | bytes 1572872 | tf_op jit(solution)/shard_map/ppermute | solution.py:11
  40.9 21.6 %collective-permute-done.9.refs_2_ = bf16[2,32,16,256]{3,2,1,0:T(8,128)(2,1)S(1)} collective-permute-done((bf16[2,32,16,256]{3,2,1,0:T(8,128)(2,1)}, bf16[2,32,16,256]{3,2,1,0:T(8,128)(2,1)S(1)}, u32[]{:S(2)}, u32[]{:S(2)}) %collective-permute-start.9) | collective-permute-done | bytes 524320 | tf_op jit(solution)/shard_map/ppermute | solution.py:11
  63.3 7.3 %collective-permute-done.10.refs_3_ = bf16[2,32,16,256]{3,2,1,0:T(8,128)(2,1)S(1)} collective-permute-done((bf16[2,32,16,256]{3,2,1,0:T(8,128)(2,1)}, bf16[2,32,16,256]{3,2,1,0:T(8,128)(2,1)S(1)}, u32[]{:S(2)}, u32[]{:S(2)}) %collective-permute-start.10) | collective-permute-done | bytes 524320 | tf_op jit(solution)/shard_map/ppermute | solution.py:11
  71.8 28.4 %collective-permute-done.12.refs_5_ = bf16[2,32,16,256]{3,2,1,0:T(8,128)(2,1)S(1)} collective-permute-done((bf16[2,32,16,256]{3,2,1,0:T(8,128)(2,1)}, bf16[2,32,16,256]{3,2,1,0:T(8,128)(2,1)S(1)}, u32[]{:S(2)}, u32[]{:S(2)}) %collective-permute-start.12) | collective-permute-done | bytes 524320 | tf_op jit(solution)/shard_map/ppermute | solution.py:11
  102.7 2.6 %collective-permute-start.18 = (bf16[2,32,16,256]{3,2,1,0:T(8,128)(2,1)S(1)}, bf16[2,32,16,256]{3,2,1,0:T(8,128)(2,1)}, u32[]{:S(2)}, u32[]{:S(2)}) collective-permute-start(bf16[2,32,16,256]{3,2,1,0:T(8,128)(2,1)S(1)} %collective-permute-done.10.refs_3_), channel_id=1, source_target_pairs={{0,24},{8,0},{16,8},{24,16},{1,25},{9,1},{17,9},{25,17},{2,26},{10... | collective-permute-start | bytes 1572872 | tf_op jit(solution)/shard_map/ppermute | solution.py:16
  105.6 1.3 collective-permute-done.17.refs_10_
  106.8 2.0 %collective-permute-start.22 = (bf16[2,32,16,256]{3,2,1,0:T(8,128)(2,1)}, bf16[2,32,16,256]{3,2,1,0:T(8,128)(2,1)}, u32[]{:S(2)}, u32[]{:S(2)}) collective-permute-start(bf16[2,32,16,256]{3,2,1,0:T(8,128)(2,1)} %collective-permute-done.14.refs_7_), channel_id=1, source_target_pairs={{0,24},{8,0},{16,8},{24,16},{1,25},{9,1},{17,9},{25,17},{2,26},{10... | collective-permute-start | bytes 1572872 | tf_op jit(solution)/shard_map/ppermute | solution.py:16
  110.2 2.3 %collective-permute-done.18.refs_11_ = bf16[2,32,16,256]{3,2,1,0:T(8,128)(2,1)} collective-permute-done((bf16[2,32,16,256]{3,2,1,0:T(8,128)(2,1)S(1)}, bf16[2,32,16,256]{3,2,1,0:T(8,128)(2,1)}, u32[]{:S(2)}, u32[]{:S(2)}) %collective-permute-start.18) | collective-permute-done | bytes 524320 | tf_op jit(solution)/shard_map/ppermute | solution.py:16
  112.5 5.6 %collective-permute-done.19.refs_12_ = bf16[2,32,16,256]{3,2,1,0:T(8,128)(2,1)} collective-permute-done((bf16[2,32,16,256]{3,2,1,0:T(8,128)(2,1)S(1)}, bf16[2,32,16,256]{3,2,1,0:T(8,128)(2,1)}, u32[]{:S(2)}, u32[]{:S(2)}) %collective-permute-start.19) | collective-permute-done | bytes 524320 | tf_op jit(solution)/shard_map/ppermute | solution.py:16
  118.1 5.6 %collective-permute-done.20.refs_13_ = bf16[2,32,16,256]{3,2,1,0:T(8,128)(2,1)} collective-permute-done((bf16[2,32,16,256]{3,2,1,0:T(8,128)(2,1)S(1)}, bf16[2,32,16,256]{3,2,1,0:T(8,128)(2,1)}, u32[]{:S(2)}, u32[]{:S(2)}) %collective-permute-start.20) | collective-permute-done | bytes 524320 | tf_op jit(solution)/shard_map/ppermute | solution.py:16
  123.7 5.7 %collective-permute-done.21.refs_14_ = bf16[2,32,16,256]{3,2,1,0:T(8,128)(2,1)} collective-permute-done((bf16[2,32,16,256]{3,2,1,0:T(8,128)(2,1)}, bf16[2,32,16,256]{3,2,1,0:T(8,128)(2,1)}, u32[]{:S(2)}, u32[]{:S(2)}) %collective-permute-start.21) | collective-permute-done | bytes 524320 | tf_op jit(solution)/shard_map/ppermute | solution.py:16
  129.4 5.4 %shard_map.62 = (f32[512,256]{1,0:T(8,128)S(1)}, bf16[512,1024]{1,0:T(8,128)(2,1)S(1)}) custom-call(s32[256]{0:T(256)S(1)} %select_reduce_fusion.ket_of_ref, bf16[2,32,16,256]{3,2,1,0:T(8,128)(2,1)S(1)} %get-tuple-element.25.refs_0_, bf16[2,32,16,256]{3,2,1,0:T(8,128)(2,1)S(1)} %collective-permute-done.8.refs_1_, ...), custom_call_target="tpu_custom_call" | custom-call | flops 1879048192 | bytes 1048576 | tf_op jit(solution)/shard_map/pallas_call | solution.py:160
  135.0 1.5 shard_map.63
  136.7 10.5 %collective-permute-start.24 = (f32[4,32,256]{2,1,0:T(8,128)S(1)}, f32[4,32,256]{2,1,0:T(8,128)S(1)}, u32[]{:S(2)}, u32[]{:S(2)}) collective-permute-start(f32[4,32,256]{2,1,0:T(8,128)S(1)} %get-tuple-element.38), channel_id=1, source_target_pairs={{0,2},{1,3},{2,0},{3,1},{4,6},{5,7},{6,4},{7,5},{8,10},{9,11},{10,... | collective-permute-start | bytes 393224 | tf_op jit(solution)/shard_map/ppermute | solution.py:11
  147.2 3.5 %collective-permute-done.24.refs_3_ = f32[4,32,256]{2,1,0:T(8,128)S(1)} collective-permute-done((f32[4,32,256]{2,1,0:T(8,128)S(1)}, f32[4,32,256]{2,1,0:T(8,128)S(1)}, u32[]{:S(2)}, u32[]{:S(2)}) %collective-permute-start.24) | collective-permute-done | bytes 131104 | tf_op jit(solution)/shard_map/ppermute | solution.py:11
  150.8 2.4 %collective-permute-start.25 = (f32[2,32,256]{2,1,0:T(8,128)S(1)}, f32[2,32,256]{2,1,0:T(8,128)S(1)}, u32[]{:S(2)}, u32[]{:S(2)}) collective-permute-start(f32[2,32,256]{2,1,0:T(8,128)S(1)} %get-tuple-element.41), channel_id=1, source_target_pairs={{0,2},{1,3},{2,0},{3,1},{4,6},{5,7},{6,4},{7,5},{8,10},{9,11},{10,... | collective-permute-start | bytes 196616 | tf_op jit(solution)/shard_map/ppermute | solution.py:11
  153.1 1.4 collective-permute-start.26
  154.5 1.2 collective-permute-done.25.refs_2_
  155.8 1.6 collective-permute-done.26.refs_3_
  157.4 2.1 %collective-permute-start.27 = (f32[2,1,32,256]{3,2,1,0:T(8,128)S(1)}, f32[2,1,32,256]{3,2,1,0:T(8,128)S(1)}, u32[]{:S(2)}, u32[]{:S(2)}) collective-permute-start(f32[2,1,32,256]{3,2,1,0:T(8,128)S(1)} %get-tuple-element.44), channel_id=1, source_target_pairs={{0,4},{1,5},{2,6},{3,7},{4,0},{5,1},{6,2},{7,3},{8,12},{9,13},{10,... | collective-permute-start | bytes 196616 | tf_op jit(solution)/shard_map/ppermute | solution.py:11
  159.5 3.8 %collective-permute-done.27 = f32[2,1,32,256]{3,2,1,0:T(8,128)S(1)} collective-permute-done((f32[2,1,32,256]{3,2,1,0:T(8,128)S(1)}, f32[2,1,32,256]{3,2,1,0:T(8,128)S(1)}, u32[]{:S(2)}, u32[]{:S(2)}) %collective-permute-start.27) | collective-permute-done | bytes 65568 | tf_op jit(solution)/shard_map/ppermute | solution.py:11
  (59 shorter events, 16.5 us)
Async XLA Ops:
  1.4 20.1 %collective-permute-start = (s32[97]{0:T(128)S(1)}, s32[97]{0:T(128)S(1)}, u32[]{:S(2)}, u32[]{:S(2)}) collective-permute-start(s32[97]{0:T(128)S(1)} %bitcast.16), channel_id=1, source_target_pairs={{0,1},{1,0},{2,3},{3,2},{4,5},{5,4},{6,7},{7,6},{8,9},{9,8},{10,11... | collective-permute-start | bytes 1172 | tf_op jit(solution)/shard_map/ppermute | solution.py:11
  4.4 20.8 %collective-permute-start.1 = (s32[97]{0:T(128)S(1)}, s32[97]{0:T(128)S(1)}, u32[]{:S(2)}, u32[]{:S(2)}) collective-permute-start(s32[97]{0:T(128)S(1)} %bitcast.17), channel_id=1, source_target_pairs={{0,2},{1,3},{2,0},{3,1},{4,6},{5,7},{6,4},{7,5},{8,10},{9,11},{10,... | collective-permute-start | bytes 1172 | tf_op jit(solution)/shard_map/ppermute | solution.py:11
  6.0 19.3 %collective-permute-start.2 = (s32[97]{0:T(128)S(1)}, s32[97]{0:T(128)S(1)}, u32[]{:S(2)}, u32[]{:S(2)}) collective-permute-start(s32[97]{0:T(128)S(1)} %bitcast.18), channel_id=1, source_target_pairs={{0,3},{1,2},{2,1},{3,0},{4,7},{5,6},{6,5},{7,4},{8,11},{9,10},{10,... | collective-permute-start | bytes 1172 | tf_op jit(solution)/shard_map/ppermute | solution.py:11
  6.0 20.9 %collective-permute-start.3 = (s32[97]{0:T(128)S(1)}, s32[97]{0:T(128)S(1)}, u32[]{:S(2)}, u32[]{:S(2)}) collective-permute-start(s32[97]{0:T(128)S(1)} %bitcast.19), channel_id=1, source_target_pairs={{0,4},{1,5},{2,6},{3,7},{4,0},{5,1},{6,2},{7,3},{8,12},{9,13},{10,... | collective-permute-start | bytes 1172 | tf_op jit(solution)/shard_map/ppermute | solution.py:11
  9.0 17.9 %collective-permute-start.4 = (s32[97]{0:T(128)S(1)}, s32[97]{0:T(128)S(1)}, u32[]{:S(2)}, u32[]{:S(2)}) collective-permute-start(s32[97]{0:T(128)S(1)} %bitcast.20), channel_id=1, source_target_pairs={{0,5},{1,4},{2,7},{3,6},{4,1},{5,0},{6,3},{7,2},{8,13},{9,12},{10,... | collective-permute-start | bytes 1172 | tf_op jit(solution)/shard_map/ppermute | solution.py:11
  15.1 0.8 copy-start
  15.9 0.8 copy-start.1
  16.8 0.8 copy-start.2
  21.5 7.2 %collective-permute-start.5 = (s32[97]{0:T(128)S(1)}, s32[97]{0:T(128)S(1)}, u32[]{:S(2)}, u32[]{:S(2)}) collective-permute-start(s32[97]{0:T(128)S(1)} %bitcast.21), channel_id=1, source_target_pairs={{0,6},{1,7},{2,4},{3,5},{4,2},{5,3},{6,0},{7,1},{8,14},{9,15},{10,... | collective-permute-start | bytes 1172 | tf_op jit(solution)/shard_map/ppermute | solution.py:11
  25.2 6.4 %collective-permute-start.6 = (s32[97]{0:T(128)S(1)}, s32[97]{0:T(128)S(1)}, u32[]{:S(2)}, u32[]{:S(2)}) collective-permute-start(s32[97]{0:T(128)S(1)} %bitcast.22), channel_id=1, source_target_pairs={{0,7},{1,6},{2,5},{3,4},{4,3},{5,2},{6,1},{7,0},{8,15},{9,14},{10,... | collective-permute-start | bytes 1172 | tf_op jit(solution)/shard_map/ppermute | solution.py:11
  25.3 12.2 %collective-permute-start.8 = (bf16[2,32,16,256]{3,2,1,0:T(8,128)(2,1)}, bf16[2,32,16,256]{3,2,1,0:T(8,128)(2,1)S(1)}, u32[]{:S(2)}, u32[]{:S(2)}) collective-permute-start(bf16[2,32,16,256]{3,2,1,0:T(8,128)(2,1)} %get-tuple-element.26), channel_id=1, source_target_pairs={{0,1},{1,0},{2,3},{3,2},{4,5},{5,4},{6,7},{7,6},{8,9},{9,8},{10,11... | collective-permute-start | bytes 1572872 | tf_op jit(solution)/shard_map/ppermute | solution.py:11
  26.9 35.7 %collective-permute-start.9 = (bf16[2,32,16,256]{3,2,1,0:T(8,128)(2,1)}, bf16[2,32,16,256]{3,2,1,0:T(8,128)(2,1)S(1)}, u32[]{:S(2)}, u32[]{:S(2)}) collective-permute-start(bf16[2,32,16,256]{3,2,1,0:T(8,128)(2,1)} %get-tuple-element.27), channel_id=1, source_target_pairs={{0,2},{1,3},{2,0},{3,1},{4,6},{5,7},{6,4},{7,5},{8,10},{9,11},{10,... | collective-permute-start | bytes 1572872 | tf_op jit(solution)/shard_map/ppermute | solution.py:11
  26.9 43.7 %collective-permute-start.10 = (bf16[2,32,16,256]{3,2,1,0:T(8,128)(2,1)}, bf16[2,32,16,256]{3,2,1,0:T(8,128)(2,1)S(1)}, u32[]{:S(2)}, u32[]{:S(2)}) collective-permute-start(bf16[2,32,16,256]{3,2,1,0:T(8,128)(2,1)} %get-tuple-element.28), channel_id=1, source_target_pairs={{0,3},{1,2},{2,1},{3,0},{4,7},{5,6},{6,5},{7,4},{8,11},{9,10},{10,... | collective-permute-start | bytes 1572872 | tf_op jit(solution)/shard_map/ppermute | solution.py:11
  28.8 41.9 %collective-permute-start.11 = (bf16[2,32,16,256]{3,2,1,0:T(8,128)(2,1)}, bf16[2,32,16,256]{3,2,1,0:T(8,128)(2,1)S(1)}, u32[]{:S(2)}, u32[]{:S(2)}) collective-permute-start(bf16[2,32,16,256]{3,2,1,0:T(8,128)(2,1)} %get-tuple-element.29), channel_id=1, source_target_pairs={{0,4},{1,5},{2,6},{3,7},{4,0},{5,1},{6,2},{7,3},{8,12},{9,13},{10,... | collective-permute-start | bytes 1572872 | tf_op jit(solution)/shard_map/ppermute | solution.py:11
  32.2 1.4 collective-permute-start.7
  33.6 66.6 %collective-permute-start.12 = (bf16[2,32,16,256]{3,2,1,0:T(8,128)(2,1)}, bf16[2,32,16,256]{3,2,1,0:T(8,128)(2,1)S(1)}, u32[]{:S(2)}, u32[]{:S(2)}) collective-permute-start(bf16[2,32,16,256]{3,2,1,0:T(8,128)(2,1)} %copy-done.2), channel_id=1, source_target_pairs={{0,5},{1,4},{2,7},{3,6},{4,1},{5,0},{6,3},{7,2},{8,13},{9,12},{10,... | collective-permute-start | bytes 1572872 | tf_op jit(solution)/shard_map/ppermute | solution.py:11
  37.5 65.2 %collective-permute-start.13 = (bf16[2,32,16,256]{3,2,1,0:T(8,128)(2,1)}, bf16[2,32,16,256]{3,2,1,0:T(8,128)(2,1)}, u32[]{:S(2)}, u32[]{:S(2)}) collective-permute-start(bf16[2,32,16,256]{3,2,1,0:T(8,128)(2,1)} %copy-done.1), channel_id=1, source_target_pairs={{0,6},{1,7},{2,4},{3,5},{4,2},{5,3},{6,0},{7,1},{8,14},{9,15},{10,... | collective-permute-start | bytes 1572872 | tf_op jit(solution)/shard_map/ppermute | solution.py:11
  62.6 42.8 %collective-permute-start.14 = (bf16[2,32,16,256]{3,2,1,0:T(8,128)(2,1)}, bf16[2,32,16,256]{3,2,1,0:T(8,128)(2,1)}, u32[]{:S(2)}, u32[]{:S(2)}) collective-permute-start(bf16[2,32,16,256]{3,2,1,0:T(8,128)(2,1)} %copy-done), channel_id=1, source_target_pairs={{0,7},{1,6},{2,5},{3,4},{4,3},{5,2},{6,1},{7,0},{8,15},{9,14},{10,... | collective-permute-start | bytes 1572872 | tf_op jit(solution)/shard_map/ppermute | solution.py:11
  70.6 34.8 %collective-permute-start.15 = (bf16[2,32,16,256]{3,2,1,0:T(8,128)(2,1)S(1)}, bf16[2,32,16,256]{3,2,1,0:T(8,128)(2,1)}, u32[]{:S(2)}, u32[]{:S(2)}) collective-permute-start(bf16[2,32,16,256]{3,2,1,0:T(8,128)(2,1)S(1)} %get-tuple-element.25.refs_0_), channel_id=1, source_target_pairs={{0,24},{8,0},{16,8},{24,16},{1,25},{9,1},{17,9},{25,17},{2,26},{10... | collective-permute-start | bytes 1572872 | tf_op jit(solution)/shard_map/ppermute | solution.py:16
  70.6 34.8 %collective-permute-start.16 = (bf16[2,32,16,256]{3,2,1,0:T(8,128)(2,1)S(1)}, bf16[2,32,16,256]{3,2,1,0:T(8,128)(2,1)}, u32[]{:S(2)}, u32[]{:S(2)}) collective-permute-start(bf16[2,32,16,256]{3,2,1,0:T(8,128)(2,1)S(1)} %collective-permute-done.8.refs_1_), channel_id=1, source_target_pairs={{0,24},{8,0},{16,8},{24,16},{1,25},{9,1},{17,9},{25,17},{2,26},{10... | collective-permute-start | bytes 1572872 | tf_op jit(solution)/shard_map/ppermute | solution.py:16
  100.1 6.7 %collective-permute-start.17 = (bf16[2,32,16,256]{3,2,1,0:T(8,128)(2,1)S(1)}, bf16[2,32,16,256]{3,2,1,0:T(8,128)(2,1)}, u32[]{:S(2)}, u32[]{:S(2)}) collective-permute-start(bf16[2,32,16,256]{3,2,1,0:T(8,128)(2,1)S(1)} %collective-permute-done.9.refs_2_), channel_id=1, source_target_pairs={{0,24},{8,0},{16,8},{24,16},{1,25},{9,1},{17,9},{25,17},{2,26},{10... | collective-permute-start | bytes 1572872 | tf_op jit(solution)/shard_map/ppermute | solution.py:16
  102.7 9.8 %collective-permute-start.18 = (bf16[2,32,16,256]{3,2,1,0:T(8,128)(2,1)S(1)}, bf16[2,32,16,256]{3,2,1,0:T(8,128)(2,1)}, u32[]{:S(2)}, u32[]{:S(2)}) collective-permute-start(bf16[2,32,16,256]{3,2,1,0:T(8,128)(2,1)S(1)} %collective-permute-done.10.refs_3_), channel_id=1, source_target_pairs={{0,24},{8,0},{16,8},{24,16},{1,25},{9,1},{17,9},{25,17},{2,26},{10... | collective-permute-start | bytes 1572872 | tf_op jit(solution)/shard_map/ppermute | solution.py:16
  105.3 12.7 %collective-permute-start.19 = (bf16[2,32,16,256]{3,2,1,0:T(8,128)(2,1)S(1)}, bf16[2,32,16,256]{3,2,1,0:T(8,128)(2,1)}, u32[]{:S(2)}, u32[]{:S(2)}) collective-permute-start(bf16[2,32,16,256]{3,2,1,0:T(8,128)(2,1)S(1)} %collective-permute-done.11.refs_4_), channel_id=1, source_target_pairs={{0,24},{8,0},{16,8},{24,16},{1,25},{9,1},{17,9},{25,17},{2,26},{10... | collective-permute-start | bytes 1572872 | tf_op jit(solution)/shard_map/ppermute | solution.py:16
  105.4 18.3 %collective-permute-start.20 = (bf16[2,32,16,256]{3,2,1,0:T(8,128)(2,1)S(1)}, bf16[2,32,16,256]{3,2,1,0:T(8,128)(2,1)}, u32[]{:S(2)}, u32[]{:S(2)}) collective-permute-start(bf16[2,32,16,256]{3,2,1,0:T(8,128)(2,1)S(1)} %collective-permute-done.12.refs_5_), channel_id=1, source_target_pairs={{0,24},{8,0},{16,8},{24,16},{1,25},{9,1},{17,9},{25,17},{2,26},{10... | collective-permute-start | bytes 1572872 | tf_op jit(solution)/shard_map/ppermute | solution.py:16
  105.5 23.9 %collective-permute-start.21 = (bf16[2,32,16,256]{3,2,1,0:T(8,128)(2,1)}, bf16[2,32,16,256]{3,2,1,0:T(8,128)(2,1)}, u32[]{:S(2)}, u32[]{:S(2)}) collective-permute-start(bf16[2,32,16,256]{3,2,1,0:T(8,128)(2,1)} %collective-permute-done.13.refs_6_), channel_id=1, source_target_pairs={{0,24},{8,0},{16,8},{24,16},{1,25},{9,1},{17,9},{25,17},{2,26},{10... | collective-permute-start | bytes 1572872 | tf_op jit(solution)/shard_map/ppermute | solution.py:16
  106.8 28.2 %collective-permute-start.22 = (bf16[2,32,16,256]{3,2,1,0:T(8,128)(2,1)}, bf16[2,32,16,256]{3,2,1,0:T(8,128)(2,1)}, u32[]{:S(2)}, u32[]{:S(2)}) collective-permute-start(bf16[2,32,16,256]{3,2,1,0:T(8,128)(2,1)} %collective-permute-done.14.refs_7_), channel_id=1, source_target_pairs={{0,24},{8,0},{16,8},{24,16},{1,25},{9,1},{17,9},{25,17},{2,26},{10... | collective-permute-start | bytes 1572872 | tf_op jit(solution)/shard_map/ppermute | solution.py:16
  136.6 10.6 %collective-permute-start.23 = (f32[4,32,256]{2,1,0:T(8,128)S(1)}, f32[4,32,256]{2,1,0:T(8,128)S(1)}, u32[]{:S(2)}, u32[]{:S(2)}) collective-permute-start(f32[4,32,256]{2,1,0:T(8,128)S(1)} %get-tuple-element.37), channel_id=1, source_target_pairs={{0,1},{1,0},{2,3},{3,2},{4,5},{5,4},{6,7},{7,6},{8,9},{9,8},{10,11... | collective-permute-start | bytes 393224 | tf_op jit(solution)/shard_map/ppermute | solution.py:11
  136.7 14.0 %collective-permute-start.24 = (f32[4,32,256]{2,1,0:T(8,128)S(1)}, f32[4,32,256]{2,1,0:T(8,128)S(1)}, u32[]{:S(2)}, u32[]{:S(2)}) collective-permute-start(f32[4,32,256]{2,1,0:T(8,128)S(1)} %get-tuple-element.38), channel_id=1, source_target_pairs={{0,2},{1,3},{2,0},{3,1},{4,6},{5,7},{6,4},{7,5},{8,10},{9,11},{10,... | collective-permute-start | bytes 393224 | tf_op jit(solution)/shard_map/ppermute | solution.py:11
  150.8 5.0 %collective-permute-start.25 = (f32[2,32,256]{2,1,0:T(8,128)S(1)}, f32[2,32,256]{2,1,0:T(8,128)S(1)}, u32[]{:S(2)}, u32[]{:S(2)}) collective-permute-start(f32[2,32,256]{2,1,0:T(8,128)S(1)} %get-tuple-element.41), channel_id=1, source_target_pairs={{0,2},{1,3},{2,0},{3,1},{4,6},{5,7},{6,4},{7,5},{8,10},{9,11},{10,... | collective-permute-start | bytes 196616 | tf_op jit(solution)/shard_map/ppermute | solution.py:11
  153.1 4.3 %collective-permute-start.26 = (f32[2,32,256]{2,1,0:T(8,128)S(1)}, f32[2,32,256]{2,1,0:T(8,128)S(1)}, u32[]{:S(2)}, u32[]{:S(2)}) collective-permute-start(f32[2,32,256]{2,1,0:T(8,128)S(1)} %get-tuple-element.42), channel_id=1, source_target_pairs={{0,1},{1,0},{2,3},{3,2},{4,5},{5,4},{6,7},{7,6},{8,9},{9,8},{10,11... | collective-permute-start | bytes 196616 | tf_op jit(solution)/shard_map/ppermute | solution.py:11
  157.4 5.9 %collective-permute-start.27 = (f32[2,1,32,256]{3,2,1,0:T(8,128)S(1)}, f32[2,1,32,256]{3,2,1,0:T(8,128)S(1)}, u32[]{:S(2)}, u32[]{:S(2)}) collective-permute-start(f32[2,1,32,256]{3,2,1,0:T(8,128)S(1)} %get-tuple-element.44), channel_id=1, source_target_pairs={{0,4},{1,5},{2,6},{3,7},{4,0},{5,1},{6,2},{7,3},{8,12},{9,13},{10,... | collective-permute-start | bytes 196616 | tf_op jit(solution)/shard_map/ppermute | solution.py:11
